TPU v7x, 32 devices: a whole 2x2x4 slice. The times are simulated.
32 devices in a mesh: clip: 8 (over z, x), frame: 4 (over y, core).
Axes of the slice: x: 2, y: 2, z: 4, core: 2. Of those that a mesh axis runs over, the one named last changes fastest.
Arguments:
- patches: bfloat16 [16, 4, 256, 768], P('clip', 'frame'), may hold values from -6 to 6
- mask_ids: int32 [16, 4, 256], P('clip', 'frame'), may hold values 0 or 1
- action_ids: int32 [16, 4], P('clip', 'frame'), may hold values from 0 to 255
- action_table: bfloat16 [256, 768], replicated, may hold values from -6 to 6
- action_proj: bfloat16 [768, 768], replicated, may hold values from -0.21875 to 0.21875
- mask_embed: float32 [768], replicated, may hold values from -6 to 6
- norm_gain: float32 [2, 2, 768], replicated, may hold values from 0.5 to 1.5
- norm_bias: float32 [2, 2, 768], replicated, may hold values from -3 to 3
- w_qkv: bfloat16 [2, 768, 2304], replicated, may hold values from -0.21875 to 0.21875
- qv_bias: float32 [2, 2, 768], replicated, may hold values from -3 to 3
- w_out: bfloat16 [2, 768, 768], replicated, may hold values from -0.875 to 0.875
- out_bias: float32 [2, 768], replicated, may hold values from -3 to 3
- w_fc1: bfloat16 [2, 768, 3072], replicated, may hold values from -0.21875 to 0.21875
- fc1_bias: float32 [2, 3072], replicated, may hold values from -3 to 3
- w_fc2: bfloat16 [2, 3072, 768], replicated, may hold values from -0.109375 to 0.109375
- fc2_bias: float32 [2, 768], replicated, may hold values from -3 to 3
- cotangent: bfloat16 [16, 4, 256, 768], P('clip', 'frame'), may hold values from -6 to 6
Outputs:
- output: bfloat16 [16, 4, 256, 768], P('clip', 'frame')
- patches_grad: bfloat16 [16, 4, 256, 768], P('clip', 'frame')
- action_table_grad: float32 [256, 768], P('clip', 'frame')
- action_proj_grad: float32 [768, 768], P('clip', 'frame')
- mask_embed_grad: float32 [768], replicated
- norm_gain_grad: float32 [2, 2, 768], replicated
- norm_bias_grad: float32 [2, 2, 768], replicated
- w_qkv_grad: float32 [2, 768, 2304], P(None, 'clip', 'frame')
- qv_bias_grad: float32 [2, 2, 768], replicated
- w_out_grad: float32 [2, 768, 768], P(None, 'clip', 'frame')
- out_bias_grad: float32 [2, 768], replicated
- w_fc1_grad: float32 [2, 768, 3072], P(None, 'clip', 'frame')
- fc1_bias_grad: float32 [2, 3072], replicated
- w_fc2_grad: float32 [2, 3072, 768], P(None, 'clip', 'frame')
- fc2_bias_grad: float32 [2, 768], replicated
All inputs are finite; a program needn't handle non-finite values. No bound on the sum of `mask_ids` on one device may be relied on, other than what follows from the above.
Results may differ from a plain program's by a relative error of at most 0.018.
Values may be sent and summed in bfloat16 or wider, within the bound.
A program may use at most 192 MiB of HBM per device.

v0:
```python
import jax
import jax.numpy as jnp
from jax import lax
from jax.sharding import PartitionSpec as P

HEADS = 12
GRID = 16
TUBE_W = 4
TUBES = 16


epsilon = 1e-06
highest = lax.Precision.HIGHEST


def layer_norm(stream, scaling, offset):
    average = jnp.mean(stream, axis=-1, keepdims=True)
    centered = stream - average
    variance = jnp.mean(centered * centered, axis=-1, keepdims=True)
    return centered * lax.rsqrt(variance + epsilon) * scaling + offset


def tube_order(hidden):
    clips, frames, model_width = (hidden.shape[0], hidden.shape[1], hidden.shape[-1])
    blocks = GRID // TUBE_W
    shaped = hidden.reshape(clips, frames, blocks, TUBE_W, blocks, TUBE_W, model_width)
    shaped = jnp.transpose(shaped, (0, 2, 4, 1, 3, 5, 6))
    return shaped.reshape(clips, blocks * blocks, frames, TUBE_W * TUBE_W, model_width)


def frame_order(grouped):
    clips, frames, model_width = (grouped.shape[0], grouped.shape[2], grouped.shape[-1])
    blocks = GRID // TUBE_W
    shaped = grouped.reshape(clips, blocks, blocks, frames, TUBE_W, TUBE_W, model_width)
    shaped = jnp.transpose(shaped, (0, 3, 1, 4, 2, 5, 6))
    return shaped.reshape(clips, frames, GRID * GRID, model_width)


def split_heads(array):
    return array.reshape(array.shape[0], array.shape[1], HEADS, array.shape[2] // HEADS)


def attend(queries, key_rows, value_rows):
    groups, length, model_width = queries.shape
    scaling = (model_width // HEADS) ** (-0.5)
    scores = (
        jnp.einsum(
            "glhe,gmhe->ghlm",
            split_heads(queries),
            split_heads(key_rows),
            preferred_element_type=jnp.float32,
        )
        * scaling
    )
    largest = jnp.max(scores, axis=-1, keepdims=True)
    expsum = jnp.exp(scores - largest)
    row_total = jnp.sum(expsum, axis=-1, keepdims=True)
    weights = (expsum / row_total).astype(jnp.bfloat16)
    mixed = jnp.einsum(
        "ghlm,gmhe->glhe", weights, split_heads(value_rows), preferred_element_type=jnp.float32
    )
    return (mixed.reshape(groups, length, model_width), largest + jnp.log(row_total))


def attend_back(queries, key_rows, value_rows, log_total, grad_mixed):
    groups, length, model_width = queries.shape
    scaling = (model_width // HEADS) ** (-0.5)
    query_heads = split_heads(queries)
    key_heads = split_heads(key_rows)
    grad_heads = split_heads(grad_mixed)
    scores = (
        jnp.einsum("glhe,gmhe->ghlm", query_heads, key_heads, preferred_element_type=jnp.float32)
        * scaling
    )
    probs_full = jnp.exp(scores - log_total)
    grad_weights = jnp.einsum(
        "glhe,gmhe->ghlm", grad_heads, split_heads(value_rows), preferred_element_type=jnp.float32
    )
    value_grad = jnp.einsum(
        "ghlm,glhe->gmhe",
        probs_full.astype(jnp.bfloat16),
        grad_heads,
        preferred_element_type=jnp.float32,
    )
    inner_sum = jnp.sum(probs_full * grad_weights, axis=-1, keepdims=True)
    score_grad = (probs_full * (grad_weights - inner_sum)).astype(jnp.bfloat16)
    query_grad = (
        jnp.einsum("ghlm,gmhe->glhe", score_grad, key_heads, preferred_element_type=jnp.float32)
        * scaling
    )
    key_grad = (
        jnp.einsum("ghlm,glhe->gmhe", score_grad, query_heads, preferred_element_type=jnp.float32)
        * scaling
    )
    return (
        query_grad.reshape(groups, length, model_width),
        key_grad.reshape(groups, length, model_width),
        value_grad.reshape(groups, length, model_width),
    )


def project_attend(grouped, qkv_weight, qv_shift):
    model_width = grouped.shape[-1]
    projected = jnp.einsum("gld,de->gle", grouped, qkv_weight, preferred_element_type=jnp.float32)
    queries = (projected[..., :model_width] + qv_shift[0]).astype(jnp.bfloat16)
    key_rows = projected[..., model_width : 2 * model_width].astype(jnp.bfloat16)
    value_rows = (projected[..., 2 * model_width :] + qv_shift[1]).astype(jnp.bfloat16)
    mixed, log_total = attend(queries, key_rows, value_rows)
    return (mixed.astype(jnp.bfloat16), queries, key_rows, value_rows, log_total)


def flatten_lead(array):
    return array.reshape((array.shape[0] * array.shape[1],) + array.shape[2:])


def block_forward(stream, weights, layer, tube):
    norm_gain, norm_bias, w_qkv, qv_bias, w_out, out_bias, w_fc1, fc1_bias, w_fc2, fc2_bias = (
        weights
    )
    clips, frames, tokens_frame, model_width = stream.shape
    hidden = layer_norm(stream, norm_gain[layer, 0], norm_bias[layer, 0]).astype(jnp.bfloat16)
    if tube:
        items = lax.all_to_all(tube_order(hidden), "frame", split_axis=1, concat_axis=2, tiled=True)
        count = items.shape[0]
        share = items.shape[1]
        tube_tokens = items.reshape(count * share, items.shape[2] * items.shape[3], items.shape[4])
        mixed_in, query_in, key_in, value_in, total_in = project_attend(
            tube_tokens, w_qkv[layer], qv_bias[layer]
        )
        mixed = flatten_lead(mixed_in.reshape((count, share) + mixed_in.shape[1:]))
        queries = flatten_lead(query_in.reshape((count, share) + query_in.shape[1:]))
        key_rows = flatten_lead(key_in.reshape((count, share) + key_in.shape[1:]))
        value_rows = flatten_lead(value_in.reshape((count, share) + value_in.shape[1:]))
        log_total = flatten_lead(total_in.reshape((count, share) + total_in.shape[1:]))
        grouped = flatten_lead(tube_tokens.reshape((count, share) + tube_tokens.shape[1:]))
        devices_frame = lax.axis_size("frame")
        outgoing = mixed.reshape(
            clips, TUBES // devices_frame, devices_frame, TUBE_W * TUBE_W, model_width
        )
        returned = lax.all_to_all(outgoing, "frame", split_axis=2, concat_axis=1, tiled=True)
        attended = frame_order(returned)
    else:
        grouped = hidden.reshape(clips * frames, tokens_frame, model_width)
        mixed, queries, key_rows, value_rows, log_total = project_attend(
            grouped, w_qkv[layer], qv_bias[layer]
        )
        attended = mixed.reshape(stream.shape)
    branch = (
        jnp.einsum("cfsd,de->cfse", attended, w_out[layer], preferred_element_type=jnp.float32)
        + out_bias[layer]
    )
    middle = stream + branch
    hidden_two = layer_norm(middle, norm_gain[layer, 1], norm_bias[layer, 1]).astype(jnp.bfloat16)
    before = (
        jnp.einsum("cfsd,dk->cfsk", hidden_two, w_fc1[layer], preferred_element_type=jnp.float32)
        + fc1_bias[layer]
    )
    activated = jax.nn.gelu(before).astype(jnp.bfloat16)
    result = (
        middle
        + jnp.einsum("cfsk,kd->cfsd", activated, w_fc2[layer], preferred_element_type=jnp.float32)
        + fc2_bias[layer]
    )
    saved = (
        grouped,
        queries,
        key_rows,
        value_rows,
        log_total,
        attended,
        middle,
        hidden_two,
        before,
        activated,
    )
    return (result, saved)


def block_backward(grad_result, stream, saved, weights, layer, tube):
    norm_gain, norm_bias, w_qkv, qv_bias, w_out, out_bias, w_fc1, fc1_bias, w_fc2, fc2_bias = (
        weights
    )
    (
        grouped,
        queries,
        key_rows,
        value_rows,
        log_total,
        attended,
        middle,
        hidden_two,
        before,
        activated,
    ) = saved
    clips, model_width = (stream.shape[0], stream.shape[-1])
    grad_low = grad_result.astype(jnp.bfloat16)
    fc2_grad = jnp.einsum("cfsk,cfsd->kd", activated, grad_low, preferred_element_type=jnp.float32)
    fc2_shift = jnp.sum(grad_low.astype(jnp.float32), axis=(0, 1, 2))
    grad_act = jnp.einsum(
        "cfsd,kd->cfsk", grad_low, w_fc2[layer], preferred_element_type=jnp.float32
    )
    grad_before = jax.vjp(jax.nn.gelu, before)[1](grad_act)[0].astype(jnp.bfloat16)
    fc1_grad = jnp.einsum(
        "cfsd,cfsk->dk", hidden_two, grad_before, preferred_element_type=jnp.float32
    )
    fc1_shift = jnp.sum(grad_before.astype(jnp.float32), axis=(0, 1, 2))
    grad_hidden_two = jnp.einsum(
        "cfsk,dk->cfsd", grad_before, w_fc1[layer], preferred_element_type=jnp.float32
    )
    norm_pull_two = jax.vjp(layer_norm, middle, norm_gain[layer, 1], norm_bias[layer, 1])[1]
    middle_part, gain_two, bias_two = norm_pull_two(grad_hidden_two)
    grad_middle = grad_result + middle_part
    grad_branch = grad_middle.astype(jnp.bfloat16)
    out_grad = jnp.einsum(
        "cfsd,cfse->de", attended, grad_branch, preferred_element_type=jnp.float32
    )
    out_shift = jnp.sum(grad_branch.astype(jnp.float32), axis=(0, 1, 2))
    grad_attended = jnp.einsum(
        "cfse,de->cfsd", grad_branch, w_out[layer], preferred_element_type=jnp.float32
    ).astype(jnp.bfloat16)
    if tube:
        devices_frame = lax.axis_size("frame")
        arrived = lax.all_to_all(
            tube_order(grad_attended), "frame", split_axis=1, concat_axis=2, tiled=True
        )
        grad_mixed = arrived.reshape(queries.shape)
    else:
        grad_mixed = grad_attended.reshape(queries.shape)
    query_grad, key_grad, value_grad = attend_back(
        queries, key_rows, value_rows, log_total, grad_mixed
    )
    query_low = query_grad.astype(jnp.bfloat16)
    value_low = value_grad.astype(jnp.bfloat16)
    packed = jnp.concatenate((query_low, key_grad.astype(jnp.bfloat16), value_low), axis=-1)
    qkv_grad = jnp.einsum("gld,gle->de", grouped, packed, preferred_element_type=jnp.float32)
    qv_shift = jnp.stack(
        (
            jnp.sum(query_low.astype(jnp.float32), axis=(0, 1)),
            jnp.sum(value_low.astype(jnp.float32), axis=(0, 1)),
        )
    )
    grad_grouped = jnp.einsum(
        "gle,de->gld", packed, w_qkv[layer], preferred_element_type=jnp.float32
    )
    if tube:
        outgoing = grad_grouped.astype(jnp.bfloat16).reshape(
            clips, TUBES // devices_frame, devices_frame, TUBE_W * TUBE_W, model_width
        )
        returned = lax.all_to_all(outgoing, "frame", split_axis=2, concat_axis=1, tiled=True)
        grad_hidden = frame_order(returned).astype(jnp.float32)
    else:
        grad_hidden = grad_grouped.reshape(stream.shape)
    norm_pull_one = jax.vjp(layer_norm, stream, norm_gain[layer, 0], norm_bias[layer, 0])[1]
    stream_part, gain_one, bias_one = norm_pull_one(grad_hidden)
    grad_stream = grad_middle + stream_part
    large = (qkv_grad, out_grad, fc1_grad, fc2_grad)
    small = (
        jnp.stack((gain_one, gain_two)),
        jnp.stack((bias_one, bias_two)),
        qv_shift,
        out_shift,
        fc1_shift,
        fc2_shift,
    )
    return (grad_stream, large, small)


def local(
    patches,
    mask_ids,
    action_ids,
    action_table,
    action_proj,
    mask_embed,
    norm_gain,
    norm_bias,
    w_qkv,
    qv_bias,
    w_out,
    out_bias,
    w_fc1,
    fc1_bias,
    w_fc2,
    fc2_bias,
    cotangent,
):
    weights = (
        norm_gain,
        norm_bias,
        w_qkv,
        qv_bias,
        w_out,
        out_bias,
        w_fc1,
        fc1_bias,
        w_fc2,
        fc2_bias,
    )
    actions = action_table.shape[0]
    onehot = (action_ids[..., None] == jnp.arange(actions, dtype=jnp.int32)).astype(jnp.bfloat16)
    chosen = jnp.einsum("cfa,ad->cfd", onehot, action_table, preferred_element_type=jnp.float32)
    drive = jnp.einsum(
        "cfd,de->cfe", chosen.astype(jnp.bfloat16), action_proj, preferred_element_type=jnp.float32
    )
    masked = mask_ids[..., None] == 1
    stream_zero = jnp.where(masked, mask_embed, patches.astype(jnp.float32)) + drive[:, :, None, :]
    stream_one, saved_one = block_forward(stream_zero, weights, 0, False)
    result, saved_two = block_forward(stream_one, weights, 1, True)
    output = result.astype(jnp.bfloat16)
    saved_two = block_forward(stream_one, weights, 1, True)[1]
    grad_one, large_two, small_two = block_backward(
        cotangent.astype(jnp.float32), stream_one, saved_two, weights, 1, True
    )
    saved_one = block_forward(stream_zero, weights, 0, False)[1]
    grad_zero, large_one, small_one = block_backward(
        grad_one, stream_zero, saved_one, weights, 0, False
    )
    embed_grad = jnp.sum(jnp.where(masked, grad_zero, 0.0), axis=(0, 1, 2))
    patch_grad = jnp.where(masked, 0.0, grad_zero).astype(jnp.bfloat16)
    drive_grad = jnp.sum(grad_zero, axis=2)
    proj_grad = jnp.einsum("cfd,cfe->de", chosen, drive_grad, precision=highest)
    chosen_grad = jnp.einsum(
        "cfe,de->cfd", drive_grad, action_proj.astype(jnp.float32), precision=highest
    )
    table_grad = jnp.einsum(
        "cfa,cfd->ad", onehot.astype(jnp.float32), chosen_grad, precision=highest
    )
    summed_rows = (
        lax.psum_scatter(
            jnp.stack((large_one[0], large_two[0])).astype(jnp.bfloat16),
            "clip",
            scatter_dimension=1,
            tiled=True,
        ).astype(jnp.float32),
        lax.psum_scatter(
            jnp.stack((large_one[1], large_two[1])).astype(jnp.bfloat16),
            "clip",
            scatter_dimension=1,
            tiled=True,
        ).astype(jnp.float32),
        lax.psum_scatter(
            jnp.stack((large_one[2], large_two[2])).astype(jnp.bfloat16),
            "clip",
            scatter_dimension=1,
            tiled=True,
        ).astype(jnp.float32),
        lax.psum_scatter(
            jnp.stack((large_one[3], large_two[3])).astype(jnp.bfloat16),
            "clip",
            scatter_dimension=1,
            tiled=True,
        ).astype(jnp.float32),
        lax.psum_scatter(
            proj_grad[None].astype(jnp.bfloat16), "clip", scatter_dimension=1, tiled=True
        ).astype(jnp.float32),
        lax.psum_scatter(
            table_grad[None].astype(jnp.bfloat16), "clip", scatter_dimension=1, tiled=True
        ).astype(jnp.float32),
    )
    summed = (
        lax.psum_scatter(
            summed_rows[0].astype(jnp.bfloat16), "frame", scatter_dimension=2, tiled=True
        ).astype(jnp.float32),
        lax.psum_scatter(
            summed_rows[1].astype(jnp.bfloat16), "frame", scatter_dimension=2, tiled=True
        ).astype(jnp.float32),
        lax.psum_scatter(
            summed_rows[2].astype(jnp.bfloat16), "frame", scatter_dimension=2, tiled=True
        ).astype(jnp.float32),
        lax.psum_scatter(
            summed_rows[3].astype(jnp.bfloat16), "frame", scatter_dimension=2, tiled=True
        ).astype(jnp.float32),
        lax.psum_scatter(
            summed_rows[4].astype(jnp.bfloat16), "frame", scatter_dimension=2, tiled=True
        ).astype(jnp.float32),
        lax.psum_scatter(
            summed_rows[5].astype(jnp.bfloat16), "frame", scatter_dimension=2, tiled=True
        ).astype(jnp.float32),
    )
    qkv_sum, out_sum, fc1_sum, fc2_sum = (summed[0], summed[1], summed[2], summed[3])
    proj_sum = summed[4][0]
    table_sum = summed[5][0]
    small = lax.psum(
        (
            jnp.stack((small_one[0], small_two[0])),
            jnp.stack((small_one[1], small_two[1])),
            jnp.stack((small_one[2], small_two[2])),
            jnp.stack((small_one[3], small_two[3])),
            jnp.stack((small_one[4], small_two[4])),
            jnp.stack((small_one[5], small_two[5])),
            embed_grad,
        ),
        ("clip", "frame"),
    )
    return (
        output,
        patch_grad,
        table_sum,
        proj_sum,
        small[6],
        small[0],
        small[1],
        qkv_sum,
        small[2],
        out_sum,
        small[3],
        fc1_sum,
        small[4],
        fc2_sum,
        small[5],
    )


def solution(mesh):
    in_specs = (
        P("clip", "frame", None, None),
        P("clip", "frame", None),
        P("clip", "frame"),
        P(),
        P(),
        P(),
        P(),
        P(),
        P(),
        P(),
        P(),
        P(),
        P(),
        P(),
        P(),
        P(),
        P("clip", "frame", None, None),
    )
    out_specs = (
        P("clip", "frame", None, None),
        P("clip", "frame", None, None),
        P("clip", "frame"),
        P("clip", "frame"),
        P(),
        P(),
        P(),
        P(None, "clip", "frame"),
        P(),
        P(None, "clip", "frame"),
        P(),
        P(None, "clip", "frame"),
        P(),
        P(None, "clip", "frame"),
        P(),
    )
    return jax.shard_map(local, mesh=mesh, in_specs=in_specs, out_specs=out_specs, check_vma=False)
```

profile of v0, /device:TPU:0, one launch (start us, length us, event | category | flops | bytes accessed | tf_op | source)
XLA Modules:
  0.0 1257.0 jit_solution(12761054243774741434)
XLA Ops:
  15.2 4.3 fusion.52
  23.6 2.6 copy.119
  34.7 2.7 fusion.29
  38.0 4.5 fusion.169
  47.2 15.7 %all_to_all.67 = bf16[2,16,1,16,768]{4,0,3,2,1:T(2,128)(2,1)S(1)} all-to-all(bf16[2,16,1,16,768]{4,0,3,2,1:T(2,128)(2,1)S(1)} %bitcast.405), channel_id=1, replica_groups=mesh['clip'=8,'frame'=4] {'frame'}, dimensions={1} | all-to-all | bytes 1572864 | tf_op jit(solution)/shard_map/all_to_all | solution.py:123
  63.0 4.3 fusion.48
  69.5 3.8 reshape.683
  73.3 3.8 reshape.685
  78.6 2.7 multiply_reduce_fusion.3
  86.3 4.3 copy.132
  90.6 3.1 convert_element_type.335
  93.7 14.2 %all_to_all.68 = bf16[2,4,4,16,768]{4,3,1,0,2:T(8,128)(2,1)S(1)} all-to-all(bf16[2,4,4,16,768]{4,3,1,0,2:T(8,128)(2,1)S(1)} %copy.133), channel_id=1, replica_groups=mesh['clip'=8,'frame'=4] {'frame'}, dimensions={2} | all-to-all | bytes 1572864 | tf_op jit(solution)/shard_map/all_to_all | solution.py:140
  109.8 2.4 fusion.170
  112.6 4.9 fusion.21
  117.5 10.6 convert_reduce_fusion
  128.1 3.4 fusion.74
  140.8 3.9 all-to-all-start.2
  146.2 10.1 all-to-all-done.2
  157.2 3.8 reshape_reshape.6
  161.0 4.9 multiply_reduce_fusion.2
  165.9 2.8 convert_reduce_fusion.2
  174.0 2.4 copy.144
  176.4 3.1 convert_element_type.346
  179.5 3.8 copy.148
  183.3 3.9 convert_element_type.349
  187.2 3.8 copy.150
  191.0 3.9 convert_element_type.353
  196.3 4.9 fusion.101
  202.7 3.5 all-to-all-start.3
  207.7 10.1 all-to-all-done.3
  220.3 2.9 reshape.697
  228.1 10.2 convert_reduce_fusion.1
  238.3 3.4 fusion.75
  247.2 2.3 copy.154
  249.5 5.9 convert_reduce_fusion.9
  265.0 2.4 copy.158
  268.7 4.8 fusion.77
  275.4 2.5 select_reduce_fusion
  281.0 3.8 fusion.94
  284.9 2.3 fusion.96
  289.7 4.1 fusion.36
  293.9 2.3 fusion.35
  296.2 3.6 pad_maximum_fusion.2
  300.9 8.7 fusion.34
  309.6 8.8 fusion.33
  318.4 8.3 pad_maximum_fusion.1
  328.1 6.6 fusion.32
  334.8 4.9 fusion.31
  339.7 8.3 pad_maximum_fusion
  350.2 60.5 %reduce-scatter.22.cloned.1.call-done = bf16[1,96,768]{2,1,0:T(8,128)(2,1)} async-done(((bf16[1,768,768]{2,1,0:T(8,128)(2,1)}), bf16[1,96,768]{2,1,0:T(8,128)(2,1)}) %reduce-scatter.22.cloned.1.call-update) | async-done | bytes 147472 | tf_op jit(solution)/shard_map/reduce_scatter | solution.py:353
  412.7 70.1 %reduce-scatter.26.cloned.1.call-done = bf16[2,96,768]{2,1,0:T(8,128)(2,1)} async-done(((bf16[2,768,768]{2,1,0:T(8,128)(2,1)}), bf16[2,96,768]{2,1,0:T(8,128)(2,1)}) %reduce-scatter.26.cloned.1.call-update) | async-done | bytes 294928 | tf_op jit(solution)/shard_map/reduce_scatter | solution.py:335
  485.1 129.6 %reduce-scatter.24.cloned.1.call-done = bf16[2,96,2304]{2,1,0:T(8,128)(2,1)} async-done(((bf16[2,768,2304]{2,1,0:T(8,128)(2,1)}), bf16[2,96,2304]{2,1,0:T(8,128)(2,1)}) %reduce-scatter.24.cloned.1.call-update) | async-done | bytes 884752 | tf_op jit(solution)/shard_map/reduce_scatter | solution.py:329
  614.7 3.7 copy.190
  618.4 3.6 reshape.723
  622.1 157.3 %reduce-scatter.32.cloned.1.call-done = bf16[2,384,768]{2,1,0:T(8,128)(2,1)} async-done(((bf16[2,3072,768]{2,1,0:T(8,128)(2,1)}), bf16[2,384,768]{2,1,0:T(8,128)(2,1)}) %reduce-scatter.32.cloned.1.call-update) | async-done | bytes 1179664 | tf_op jit(solution)/shard_map/reduce_scatter | solution.py:347
  779.4 4.7 copy.167
  785.5 158.6 %reduce-scatter.28.cloned.1.call-done = bf16[2,96,3072]{2,1,0:T(8,128)(2,1)} async-done(((bf16[2,768,3072]{2,1,0:T(8,128)(2,1)}), bf16[2,96,3072]{2,1,0:T(8,128)(2,1)}) %reduce-scatter.28.cloned.1.call-update) | async-done | bytes 1179664 | tf_op jit(solution)/shard_map/reduce_scatter | solution.py:341
  944.2 9.0 fusion.104
  981.0 7.8 reduce-scatter.36.cloned.1.call-done
  990.5 22.3 %reduce-scatter.40.cloned.1.call-done = bf16[192,192]{1,0:T(8,128)(2,1)} async-done(((bf16[768,192]{1,0:T(8,128)(2,1)}), bf16[192,192]{1,0:T(8,128)(2,1)}) %reduce-scatter.40.cloned.1.call-update) | async-done | bytes 73744
  1014.6 26.3 %reduce-scatter.38.cloned.1.call-done = bf16[576,192]{1,0:T(8,128)(2,1)} async-done(((bf16[2304,192]{1,0:T(8,128)(2,1)}), bf16[576,192]{1,0:T(8,128)(2,1)}) %reduce-scatter.38.cloned.1.call-update) | async-done | bytes 221200
  1043.0 37.8 %all-reduce.5.cloned.1.call-done = bf16[2,384,768]{1,0,2:T(2,128)(2,1)} async-done(((bf16[2,384,768]{1,0,2:T(2,128)(2,1)}), bf16[2,384,768]{1,0,2:T(2,128)(2,1)}) %all-reduce.5.cloned.1.call-update) | async-done | bytes 1179664
  1082.9 26.2 %reduce-scatter.30.cloned.1.call-done = bf16[2,96,768]{2,1,0:T(8,128)(2,1)} async-done(((bf16[2,96,3072]{2,1,0:T(8,128)(2,1)}), bf16[2,96,768]{2,1,0:T(8,128)(2,1)}) %reduce-scatter.30.cloned.1.call-update) | async-done | bytes 294928 | tf_op jit(solution)/shard_map/reduce_scatter | solution.py:367
  1110.9 130.3 %all-reduce.7.cloned.1.call-done = (f32[768]{0:T(1024)}, f32[2,2,768]{2,1,0:T(2,128)}, f32[2,2,768]{2,1,0:T(2,128)}, f32[2,2,768]{2,1,0:T(2,128)}, f32[2,768]{1,...) async-done(((f32[768]{0:T(1024)}, f32[2,2,768]{2,1,0:T(2,128)}, f32[2,2,768]{2,1,0:T(2,128)}, f32[2,2,768]{2,1,0:T(2,128)}, f32[2,768]{1,0:T(2,128)}, ...) | async-done | bytes 76816 | tf_op jit(solution)/shard_map/psum | solution.py:383
  (490 shorter events, 144.7 us)
Async XLA Ops:
  7.2 5.4 copy-start.117
  7.2 6.0 copy-start.100
  7.3 6.6 copy-start.75
  7.3 7.2 copy-start.101
  7.3 7.2 copy-start.102
  8.1 11.4 copy-start.59
  11.5 8.0 copy-start.67
  12.0 7.5 copy-start.64
  27.3 6.8 slice-start.2
  38.0 5.4 copy-start.92
  112.1 19.4 %copy-start.25 = (f32[2,1,256,768]{3,2,0,1:T(8,128)}, f32[2,1,256,768]{3,2,0,1:T(8,128)S(1)}, u32[]{:S(2)}) copy-start(f32[2,1,256,768]{3,2,0,1:T(8,128)S(1)} %get-tuple-element.120) | copy-start | bytes 4718596
  112.2 19.4 %copy-start.81 = (f32[2,256]{1,0:T(2,128)}, f32[2,256]{1,0:T(2,128)S(1)}, u32[]{:S(2)}) copy-start(f32[2,256]{1,0:T(2,128)S(1)} %broadcast_multiply_fusion) | copy-start | bytes 6148
  112.5 19.1 %copy-start.114 = (f32[2,256]{1,0:T(2,128)}, f32[2,256]{1,0:T(2,128)S(1)}, u32[]{:S(2)}) copy-start(f32[2,256]{1,0:T(2,128)S(1)} %fusion.152) | copy-start | bytes 6148
  112.5 15.6 %slice-start.5 = ((s8[9437184]{0:T(1024)(128)(4,1)}), s8[4194304]{0:T(1024)(128)(4,1)S(1)}, s32[]{:S(2)}) async-start(s8[9437184]{0:T(1024)(128)(4,1)} %bitcast.442), calls=%async_computation.33 | async-start | bytes 8388608
  117.5 10.6 copy-start.135
  117.5 10.6 slice-start.6
  117.5 10.6 slice-start.7
  140.8 15.5 %all-to-all-start.2 = ((bf16[2,16,1,16,768]{4,0,3,2,1:T(2,128)(2,1)}), bf16[2,16,1,16,768]{4,0,3,2,1:T(2,128)(2,1)S(1)}, u32[]{:S(2)}, u32[]{:S(2)}) async-start(bf16[2,16,1,16,768]{4,0,3,2,1:T(2,128)(2,1)} %bitcast.404), calls=%async_computation.2 | async-start | bytes 1572864 | tf_op jit(solution)/shard_map/all_to_all | solution.py:223
  202.7 15.1 %all-to-all-start.3 = ((bf16[2,4,4,16,768]{4,1,3,0,2:T(4,128)(2,1)}), bf16[2,4,4,16,768]{4,1,3,0,2:T(4,128)(2,1)S(1)}, u32[]{:S(2)}, u32[]{:S(2)}) async-start(bf16[2,4,4,16,768]{4,1,3,0,2:T(4,128)(2,1)} %copy.151), calls=%async_computation.3 | async-start | bytes 1572864 | tf_op jit(solution)/shard_map/all_to_all | solution.py:249
  206.2 142.1 %reduce-scatter.20.cloned.1.call-start = ((), (), s32[]{:S(2)}) async-start(), calls=%async_computation.15 | async-start | bytes 442368 | tf_op jit(solution)/shard_map/reduce_scatter | solution.py:356
  226.7 11.6 slice-start.8
  228.1 14.9 %copy-start.5 = (f32[2,1,256,768]{3,2,0,1:T(8,128)}, f32[2,1,256,768]{3,2,0,1:T(8,128)S(1)}, u32[]{:S(2)}) copy-start(f32[2,1,256,768]{3,2,0,1:T(8,128)S(1)} %get-tuple-element.94) | copy-start | bytes 4718596
  228.1 10.2 copy-start.29
  228.1 10.2 copy-start.79
  228.1 10.2 copy-start.96
  228.1 10.2 copy-start.112
  228.1 10.2 slice-start.9
  228.1 10.2 slice-start.10
  245.4 10.0 slice-start
  249.5 5.9 slice-start.1
  249.5 5.9 copy-start.17
  249.5 5.9 copy-start.33
  268.6 6.7 copy-start.13
  281.0 129.7 %reduce-scatter.22.cloned.1.call-start = ((), (), s32[]{:S(2)}) async-start(), calls=%async_computation.16 | async-start | bytes 1327104 | tf_op jit(solution)/shard_map/reduce_scatter | solution.py:353
  284.8 198.0 %reduce-scatter.26.cloned.1.call-start = ((), (), s32[]{:S(2)}) async-start(), calls=%async_computation.18 | async-start | bytes 2654208 | tf_op jit(solution)/shard_map/reduce_scatter | solution.py:335
  289.6 325.1 %reduce-scatter.24.cloned.1.call-start = ((), (), s32[]{:S(2)}) async-start(), calls=%async_computation.17 | async-start | bytes 7962624 | tf_op jit(solution)/shard_map/reduce_scatter | solution.py:329
  299.8 479.6 %reduce-scatter.32.cloned.1.call-start = ((), (), s32[]{:S(2)}) async-start(), calls=%async_computation.21 | async-start | bytes 10616832 | tf_op jit(solution)/shard_map/reduce_scatter | solution.py:347
  300.9 8.7 copy-start.110
  326.7 8.0 copy-start.80
  326.7 8.0 copy-start.97
  326.8 8.0 copy-start.113
  326.8 8.0 copy-start.119
  326.8 617.3 %reduce-scatter.28.cloned.1.call-start = ((), (), s32[]{:S(2)}) async-start(), calls=%async_computation.19 | async-start | bytes 10616832 | tf_op jit(solution)/shard_map/reduce_scatter | solution.py:341
  328.1 6.6 copy-start.30
  328.1 6.6 copy-start.139
  348.0 631.5 %reduce-scatter.34.cloned.1.call-start = ((), (), s32[]{:S(2)}) async-start(), calls=%async_computation.22 | async-start | bytes 245760
  350.1 638.7 %reduce-scatter.36.cloned.1.call-start = ((), (), s32[]{:S(2)}) async-start(), calls=%async_computation.23 | async-start | bytes 245760
  412.7 600.1 %reduce-scatter.40.cloned.1.call-start = ((), (), s32[]{:S(2)}) async-start(), calls=%async_computation.25 | async-start | bytes 491520
  485.1 555.8 %reduce-scatter.38.cloned.1.call-start = ((), (), s32[]{:S(2)}) async-start(), calls=%async_computation.24 | async-start | bytes 1474560
  622.0 162.2 %copy-start.134 = (u32[32]{0:T(128)S(1)}, u32[32]{0:T(128)}, u32[]{:S(2)}) copy-start(u32[32]{0:T(128)} %constant.52) | copy-start | bytes 388
  622.0 322.1 %copy-start.105 = (f32[1,3072]{1,0:T(1,128)S(1)}, f32[1,3072]{1,0:T(1,128)}, u32[]{:S(2)}) copy-start(f32[1,3072]{1,0:T(1,128)} %get-tuple-element.109) | copy-start | bytes 36868
  622.1 322.1 %copy-start.124 = (f32[768]{0:T(1024)S(1)}, f32[768]{0:T(1024)}, u32[]{:S(2)}) copy-start(f32[768]{0:T(1024)} %get-tuple-element.82) | copy-start | bytes 9220
  622.1 458.8 %all-reduce.5.cloned.1.call-start = ((), (), s32[]{:S(2)}) async-start(), calls=%async_computation.26 | async-start | bytes 2359296
  784.2 324.9 %reduce-scatter.30.cloned.1.call-start = ((), (), s32[]{:S(2)}) async-start(), calls=%async_computation.20 | async-start | bytes 1474560 | tf_op jit(solution)/shard_map/reduce_scatter | solution.py:367
  944.1 297.1 %all-reduce.7.cloned.1.call-start = ((), (), s32[]{:S(2)}) async-start(), calls=%async_computation.27 | async-start | bytes 155648 | tf_op jit(solution)/shard_map/psum | solution.py:383
  944.2 9.0 copy-start.127
  944.2 14.3 %copy-start.72 = (f32[12,64]{1,0:T(8,128)S(1)}, f32[12,64]{1,0:T(8,128)}, u32[]{:S(2)}) copy-start(f32[12,64]{1,0:T(8,128)} %get-tuple-element.129) | copy-start | bytes 9220
  953.2 10.8 copy-start.10
  953.8 10.9 copy-start.19
  956.0 10.5 copy-start.91
  956.0 20.6 %copy-start.63 = (pred[2,1,256]{2,0,1:T(4,128)(4,1)S(1)}, pred[2,1,256]{2,0,1:T(4,128)(4,1)}, u32[]{:S(2)}) copy-start(pred[2,1,256]{2,0,1:T(4,128)(4,1)} %copy-done.59) | copy-start | bytes 1540
  959.2 9.3 copy-start.73
  964.7 14.1 %copy-start.106 = (f32[3072]{0:T(1024)S(1)}, f32[3072]{0:T(1024)}, u32[]{:S(2)}) copy-start(f32[3072]{0:T(1024)} %get-tuple-element.137) | copy-start | bytes 36868
  964.7 14.1 %copy-start.107 = (f32[3072]{0:T(1024)S(1)}, f32[3072]{0:T(1024)}, u32[]{:S(2)}) copy-start(f32[3072]{0:T(1024)} %get-tuple-element.139) | copy-start | bytes 36868
  (105 other events, 304.3 us)
Sparse Core Ops, SparseCore 0:
  281.1 62.5 reduce-scatter.19
  347.1 63.5 reduce-scatter.21
  414.2 68.5 reduce-scatter.25
  486.3 128.3 reduce-scatter.23
  618.1 161.2 reduce-scatter.31
  782.9 161.1 reduce-scatter.27
  947.1 18.8 reduce-scatter.33
  969.0 19.7 reduce-scatter.35
  991.9 20.8 reduce-scatter.39
  1015.2 25.6 reduce-scatter.37
  1043.2 37.5 all-reduce.4
  1083.3 25.7 reduce-scatter.29
  1116.6 124.5 all-reduce.6
where the time goes:
time: 1270 us; the launch traced here: 1260 us
  waiting for transfers between devices  847 us (67%)
  matrix products  151 us (12%)
  local copies, waits for them, and re-layouts  134 us (11%)
  other arithmetic  69.8 us (5%)
  blocking collectives  29.9 us (2%)
  between operations  16.6 us (1%)
    reduce_scatter x1, waiting for transfers between devices, local(): lax.psum_scatter(jnp.stack((large_one[2], large_two[2])).astype(jnp.bfloa...  159 us
    reduce_scatter x1, waiting for transfers between devices, local(): lax.psum_scatter(jnp.stack((large_one[3], large_two[3])).astype(jnp.bfloa...  157 us
    psum x1, waiting for transfers between devices, local(): lax.psum((jnp.stack((small_one[0], small_two[0])), jnp.stack((small_one[1...  130 us
    reduce_scatter x1, waiting for transfers between devices, local(): lax.psum_scatter(jnp.stack((large_one[0], large_two[0])).astype(jnp.bfloa...  130 us
    unnamed x18, waiting for transfers between devices  94.4 us
    reduce_scatter x1, waiting for transfers between devices, local(): lax.psum_scatter(jnp.stack((large_one[1], large_two[1])).astype(jnp.bfloa...  70.1 us
    reduce_scatter x1, waiting for transfers between devices, local(): lax.psum_scatter(proj_grad[None].astype(jnp.bfloat16), 'clip', scatter_di...  60.5 us
    unnamed x336, local copies, waits for them, and re-layouts  45.8 us
  transfers between devices with their start and end apart: 15, of which 13 were waited for; matrix products, arithmetic and copies ran while one was open for 10% of the time, Pallas kernels for 0%

commit v1 on v0

v1 whole, which is shorter than its diff:
```python
import functools

import jax
import jax.numpy as jnp
from jax import lax
from jax.experimental import pallas as pl
from jax.experimental.pallas import tpu as pltpu
from jax.sharding import PartitionSpec as P

HEADS = 12
GRID = 16
TUBE_W = 4
TUBES = 16
HEAD = 64
STEP = 256

epsilon = 1e-06
highest = lax.Precision.HIGHEST
f32 = jnp.float32
bf16 = jnp.bfloat16
PARAMS = pltpu.CompilerParams(vmem_limit_bytes=60 * 1024 * 1024)


def wide(value):
    return value.astype(f32)


def narrow(value):
    return value.astype(bf16)


def dot(a, b, a_dim=1, b_dim=0):
    return lax.dot_general(a, b, (((a_dim,), (b_dim,)), ((), ())), preferred_element_type=f32)


def normalize(stream):
    centered = stream - jnp.mean(stream, axis=-1, keepdims=True)
    scale = lax.rsqrt(jnp.mean(centered * centered, axis=-1, keepdims=True) + epsilon)
    return centered * scale, scale


def normalize_back(grad, stream, gain):
    unit, scale = normalize(stream)
    inner = grad * gain
    part = scale * (
        inner
        - jnp.mean(inner, axis=-1, keepdims=True)
        - unit * jnp.mean(inner * unit, axis=-1, keepdims=True)
    )
    return part, rows_sum(grad * unit), rows_sum(grad)


def rows_sum(value):
    return jnp.sum(value, axis=0, keepdims=True)


def gelu_pair(u):
    root = 0.7978845608028654
    square = u * u
    t = jnp.tanh(root * u * (1.0 + 0.044715 * square))
    half = 0.5 * (1.0 + t)
    slope = half + 0.5 * u * (1.0 - t * t) * (root * (1.0 + 3 * 0.044715 * square))
    return u * half, slope


def softmax(scores, group):
    length = scores.shape[0]
    if group < length:
        same = (
            lax.broadcasted_iota(jnp.int32, scores.shape, 0) // group
            == lax.broadcasted_iota(jnp.int32, scores.shape, 1) // group
        )
        scores = jnp.where(same, scores, -1e30)
    expsum = jnp.exp(scores - jnp.max(scores, axis=-1, keepdims=True))
    return expsum / jnp.sum(expsum, axis=-1, keepdims=True)


def low_lanes(length):
    return lax.broadcasted_iota(jnp.int32, (length, 2 * HEAD), 1) < HEAD


def attend_kernel(*refs, first, group, tokens_frame):
    if first:
        (patches, mask, embed, drive, gain, bias, wq, wk, wv, qb, vb) = refs[:11]
        (stream, hidden, q_out, k_out, v_out, mixed) = refs[11:]

        @pl.when(pl.program_id(0) == 0)
        def _():
            for part in range(patches.shape[0] // tokens_frame):
                rows = pl.ds(part * tokens_frame, tokens_frame)
                value = jnp.where(mask[rows, :] == 1, embed[...], wide(patches[rows, :]))
                value = value + drive[pl.ds(part, 1), :]
                stream[rows, :] = value
                hidden[rows, :] = narrow(normalize(value)[0] * gain[0] + bias[0])

    else:
        hidden, wq, wk, wv, qb, vb, q_out, k_out, v_out, mixed = refs
    source = hidden[...]
    q_out[...] = narrow(dot(source, wq[0]) + qb[0])
    k_out[...] = narrow(dot(source, wk[0]))
    v_out[...] = narrow(dot(source, wv[0]) + vb[0])
    length = max(group, 128)
    lanes = low_lanes(length)
    for block in range(source.shape[0] // length):
        rows = pl.ds(block * length, length)
        for pair in range(STEP // (2 * HEAD)):
            columns = pl.ds(pair * 2 * HEAD, 2 * HEAD)
            q, k, v = q_out[rows, columns], k_out[rows, columns], v_out[rows, columns]
            results = []
            for mine in (lanes, ~lanes):
                scores = dot(jnp.where(mine, q, 0), k, 1, 1) * HEAD**-0.5
                results.append(dot(narrow(softmax(scores, group)), v))
            mixed[rows, columns] = narrow(jnp.where(lanes, results[0], results[1]))


def attend_back_kernel(*refs, first, group, tokens_frame):
    if first:
        (go, q_in, k_in, v_in, wq, wk, wv, gain, stream, gmid, mask) = refs[:11]
        (dq_out, dk_out, dv_out, shifts, patch_grad, small, total) = refs[11:]
    else:
        go, q_in, k_in, v_in, wq, wk, wv = refs[:7]
        dq_out, dk_out, dv_out, shifts, grouped, total = refs[7:]
    length = max(group, 128)
    lanes = low_lanes(length)
    for block in range(go.shape[0] // length):
        rows = pl.ds(block * length, length)
        for pair in range(STEP // (2 * HEAD)):
            columns = pl.ds(pair * 2 * HEAD, 2 * HEAD)
            q, k, v = q_in[rows, columns], k_in[rows, columns], v_in[rows, columns]
            g = go[rows, columns]
            results = []
            for mine in (lanes, ~lanes):
                scores = dot(jnp.where(mine, q, 0), k, 1, 1) * HEAD**-0.5
                probs = softmax(scores, group)
                grad = dot(jnp.where(mine, g, 0), v, 1, 1)
                inner = jnp.sum(probs * grad, axis=-1, keepdims=True)
                ds = narrow(probs * (grad - inner))
                results.append(
                    (
                        dot(ds, k) * HEAD**-0.5,
                        dot(ds, q, 0, 0) * HEAD**-0.5,
                        dot(narrow(probs), g, 0, 0),
                    )
                )
            for out, low, high in zip((dq_out, dk_out, dv_out), *results):
                out[rows, columns] = narrow(jnp.where(lanes, low, high))
    dq, dk, dv = dq_out[...], dk_out[...], dv_out[...]
    shifts[...] = jnp.zeros_like(shifts)
    shifts[0:1, :] = rows_sum(wide(dq))
    shifts[1:2, :] = rows_sum(wide(dv))
    part = dot(dq, wq[0], 1, 1) + dot(dk, wk[0], 1, 1) + dot(dv, wv[0], 1, 1)
    step = pl.program_id(0)

    @pl.when(step == 0)
    def _():
        total[...] = part

    @pl.when(step > 0)
    def _():
        total[...] += part

    @pl.when(step == pl.num_programs(0) - 1)
    def _():
        if not first:
            grouped[...] = narrow(total[...])
        else:
            back, gain_grad, bias_grad = normalize_back(total[...], stream[...], gain[0])
            zero = gmid[...] + back
            masked = mask[...] == 1
            patch_grad[...] = narrow(jnp.where(masked, 0.0, zero))
            small[...] = jnp.zeros_like(small)
            small[0:1, :] = gain_grad
            small[1:2, :] = bias_grad
            small[2:3, :] = rows_sum(jnp.where(masked, zero, 0.0))
            for frame in range(zero.shape[0] // tokens_frame):
                small[3 + frame : 4 + frame, :] = rows_sum(
                    zero[frame * tokens_frame : (frame + 1) * tokens_frame]
                )


def mlp_kernel(
    stream, mixed, w_out, out_bias, gain, bias, w_fc1, fc1_bias, w_fc2, fc2_bias, gain_next, bias_next,
    middle, hidden_two, before_out, activated_out, result, hidden,
):
    step = pl.program_id(0)

    @pl.when(step == 0)
    def _():
        value = stream[...] + dot(mixed[...], w_out[0]) + out_bias[0]
        middle[...] = value
        hidden_two[...] = narrow(normalize(value)[0] * gain[0] + bias[0])
        result[...] = value + fc2_bias[0]

    before = dot(hidden_two[...], w_fc1[0]) + fc1_bias[0]
    before_out[...] = before
    activated = narrow(gelu_pair(before)[0])
    activated_out[...] = activated
    result[...] += dot(activated, w_fc2[0])

    @pl.when(step == pl.num_programs(0) - 1)
    def _():
        hidden[...] = narrow(normalize(result[...])[0] * gain_next[0] + bias_next[0])


def mlp_tail(grad, gh2, middle, gain, w_out, gmid, gb_out, go, small):
    back, gain_grad, bias_grad = normalize_back(gh2, middle, gain)
    value = grad + back
    gmid[...] = value
    gb = narrow(value)
    gb_out[...] = gb
    go[...] = narrow(dot(gb, w_out, 1, 1))
    small[0:1, :] = gain_grad
    small[1:2, :] = bias_grad
    small[2:3, :] = rows_sum(wide(gb))


def mlp_both_kernel(
    stream, mixed, w_out, out_bias, gain, bias, w_fc1, fc1_bias, w_fc2, fc2_bias, cotangent,
    output, hidden_two, activated_out, gu_out, gmid, gb, go, small,
    middle, result, gh2,
):
    step = pl.program_id(0)

    @pl.when(step == 0)
    def _():
        value = stream[...] + dot(mixed[...], w_out[0]) + out_bias[0]
        middle[...] = value
        hidden_two[...] = narrow(normalize(value)[0] * gain[0] + bias[0])
        result[...] = value + fc2_bias[0]
        gh2[...] = jnp.zeros_like(gh2)
        small[3:4, :] = rows_sum(wide(cotangent[...]))

    before = dot(hidden_two[...], w_fc1[0]) + fc1_bias[0]
    value, slope = gelu_pair(before)
    activated = narrow(value)
    activated_out[...] = activated
    result[...] += dot(activated, w_fc2[0])
    gu = narrow(slope * dot(cotangent[...], w_fc2[0], 1, 1))
    gu_out[...] = gu
    small[pl.ds(4 + step, 1), :] = rows_sum(wide(gu))
    gh2[...] += dot(gu, w_fc1[0], 1, 1)

    @pl.when(step == pl.num_programs(0) - 1)
    def _():
        output[...] = narrow(result[...])
        mlp_tail(wide(cotangent[...]), gh2[...], middle[...], gain[0], w_out[0], gmid, gb, go, small)


def mlp_back_kernel(
    gmid_next, grad_hidden, stream_next, gain_next, middle, gain, before, w_fc1, w_fc2, w_out,
    gm, gu_out, gmid, gb, go, small, small_next,
    grad, gh2,
):
    step = pl.program_id(0)

    @pl.when(step == 0)
    def _():
        back, gain_grad, bias_grad = normalize_back(
            wide(grad_hidden[...]), stream_next[...], gain_next[0]
        )
        value = gmid_next[...] + back
        grad[...] = value
        low = narrow(value)
        gm[...] = low
        gh2[...] = jnp.zeros_like(gh2)
        small[3:4, :] = rows_sum(wide(low))
        small_next[...] = jnp.zeros_like(small_next)
        small_next[0:1, :] = gain_grad
        small_next[1:2, :] = bias_grad

    gu = narrow(gelu_pair(before[...])[1] * dot(gm[...], w_fc2[0], 1, 1))
    gu_out[...] = gu
    small[pl.ds(4 + step, 1), :] = rows_sum(wide(gu))
    gh2[...] += dot(gu, w_fc1[0], 1, 1)

    @pl.when(step == pl.num_programs(0) - 1)
    def _():
        mlp_tail(grad[...], gh2[...], middle[...], gain[0], w_out[0], gmid, gb, go, small)


def whole_spec(shape):
    return pl.BlockSpec(tuple(shape), lambda *_: (0,) * len(shape))


def vector_spec(row, width):
    return pl.BlockSpec((1, 1, width), lambda *_: (row, 0, 0))


def call(body, grid, inputs, outputs, scratch=(), flops=0):
    moved = sum(a.size * a.dtype.itemsize for a, _ in inputs) // 2
    return pl.pallas_call(
        body,
        grid=grid,
        in_specs=[s or whole_spec(a.shape) for a, s in inputs],
        out_specs=[s or whole_spec(shape) for shape, _, s in outputs],
        out_shape=[jax.ShapeDtypeStruct(shape, dtype) for shape, dtype, _ in outputs],
        scratch_shapes=list(scratch),
        compiler_params=PARAMS,
        cost_estimate=pl.CostEstimate(flops=flops, bytes_accessed=moved, transcendentals=0),
    )(*[a for a, _ in inputs])


def head_specs(w_qkv, layer):
    width = w_qkv.shape[1]
    steps = width // STEP
    return [
        (w_qkv, pl.BlockSpec((1, width, STEP), lambda i, part=part: (layer, 0, i + steps * part)))
        for part in range(3)
    ]


def column_spec(tokens):
    return pl.BlockSpec((tokens, STEP), lambda i: (0, i))


def project_attend(w_qkv, qv_bias, layer, group, start=None, hidden=None, tokens_frame=None):
    first = hidden is None
    tokens, width = (start[0] if first else hidden).shape
    inputs = [(a, None) for a in start[:4]] if first else [(hidden, None)]
    if first:
        inputs += start[4]
    inputs += head_specs(w_qkv, layer)
    flat = qv_bias.reshape(-1, 1, width)
    inputs += [
        (flat, pl.BlockSpec((1, 1, STEP), lambda i, row=2 * layer + part: (row, 0, i))) for part in range(2)
    ]
    outputs = [((tokens, width), bf16, column_spec(tokens))] * 4
    if first:
        outputs = [((tokens, width), f32, None), ((tokens, width), bf16, None)] + outputs
    body = functools.partial(attend_kernel, first=first, group=group, tokens_frame=tokens_frame)
    return call(body, (width // STEP,), inputs, outputs, flops=8 * tokens * width * width)


def project_back(go, queries, key_rows, value_rows, w_qkv, layer, group, extra=None, tokens_frame=None):
    first = extra is not None
    tokens, width = go.shape
    inputs = [(a, column_spec(tokens)) for a in (go, queries, key_rows, value_rows)]
    inputs += head_specs(w_qkv, layer)
    outputs = [((tokens, width), bf16, column_spec(tokens))] * 3
    outputs.append(((8, width), f32, pl.BlockSpec((8, STEP), lambda i: (0, i))))
    if first:
        inputs += extra
        outputs += [((tokens, width), bf16, None), ((8, width), f32, None)]
    else:
        outputs.append(((tokens, width), bf16, None))
    body = functools.partial(attend_back_kernel, first=first, group=group, tokens_frame=tokens_frame)
    return call(
        body,
        (width // STEP,),
        inputs,
        outputs,
        [pltpu.VMEM((tokens, width), f32)],
        flops=10 * tokens * width * width,
    )


def xor_permute(value, axis, flip):
    count = lax.axis_size(axis)
    return lax.ppermute(value, axis, [(i, i ^ flip) for i in range(count)])


def split_columns(arrays, count):
    width = sum(a.shape[1] for a in arrays) // count
    edges = []
    start = 0
    for a in arrays:
        edges.append((start, start + a.shape[1], a))
        start += a.shape[1]
    for block in range(count):
        low, high = block * width, (block + 1) * width
        at = 0
        for begin, end, a in edges:
            lo, hi = max(low, begin), min(high, end)
            if lo < hi:
                yield block, at, hi - lo, a, lo - begin
                at += hi - lo


def side_by_side(product, blocks, pieces):
    rows, columns = product.shape
    if pieces == 1:
        return product.reshape(blocks, rows // blocks, columns)
    cut = product.reshape(blocks, pieces, rows // blocks // pieces, columns)
    return jnp.concatenate([cut[:, i] for i in range(pieces)], axis=-1)


def store_blocks(product, unit, send, keep):
    @pl.when(pl.program_id(0) == 0)
    def _():
        send[unit, 0] = product

    @pl.when(pl.program_id(0) == 1)
    def _():
        keep[unit, 0] = product


def mlp_grad_kernel(order, hidden_two, gu, activated, gm, send, keep, held, *, blocks, count):
    rest = pl.num_programs(1)
    place = order[pl.program_id(0) * rest + pl.program_id(1)]

    @pl.when((pl.program_id(0) == 0) & (pl.program_id(1) == 0))
    def _():
        for block, at, size, a, low in split_columns((gm,), count):
            held[block, :, at : at + size] = a[:, low : low + size]

    store_blocks(narrow(side_by_side(dot(hidden_two[...], gu[...], 0, 0), blocks, 1)), 0, send, keep)
    pieces = activated.shape[1] // hidden_two.shape[1]
    store_blocks(
        narrow(side_by_side(dot(activated[...], held[place], 0, 0), blocks, pieces)), 1, send, keep
    )


def attend_grad_kernel(order, hidden, dq, dk, dv, mixed, gb, send, keep, held, held_out, *, blocks, count):
    rest = pl.num_programs(1)
    place = order[pl.program_id(0) * rest + pl.program_id(1)]

    @pl.when((pl.program_id(0) == 0) & (pl.program_id(1) == 0))
    def _():
        for block, at, size, a, low in split_columns((dq, dk, dv), count):
            held[block, :, at : at + size] = a[:, low : low + size]
        for block, at, size, a, low in split_columns((gb,), count):
            held_out[block, :, at : at + size] = a[:, low : low + size]

    one = side_by_side(dot(hidden[...], held[place], 0, 0), blocks, 1)
    two = side_by_side(dot(mixed[...], held_out[place], 0, 0), blocks, 1)
    store_blocks(narrow(jnp.concatenate((one, two), axis=-1)), 0, send, keep)


def gradient_blocks(mlp, *arrays):
    frame_size, clip_size = lax.axis_size("frame"), lax.axis_size("clip")
    rest = frame_size // 2
    frame = lax.axis_index("frame")
    core, upper = frame % 2, frame // 2
    order = jnp.stack([(upper ^ j) * 2 + (core ^ (1 - r)) for r in range(2) for j in range(rest)])
    tokens, width = arrays[0].shape
    units = 2 if mlp else 1
    shape = (units, rest, clip_size, width // clip_size, 4 * width // frame_size)
    block = (units, 1) + shape[2:]
    in_specs = [pl.BlockSpec(a.shape, lambda r, j, o: (0, 0)) for a in arrays]
    if mlp:
        gu_width = arrays[1].shape[1] // frame_size
        if gu_width % 128 == 0:
            in_specs[1] = pl.BlockSpec((tokens, gu_width), lambda r, j, o: (0, o[r * rest + j]))
        else:
            arrays = list(arrays)
            arrays[1] = jnp.transpose(arrays[1].reshape(tokens, frame_size, gu_width), (1, 0, 2))
            in_specs[1] = pl.BlockSpec(
                (pl.Squeezed(), tokens, gu_width), lambda r, j, o: (o[r * rest + j], 0, 0)
            )
        body = mlp_grad_kernel
        scratch = [pltpu.VMEM((frame_size, tokens, width // frame_size), bf16)]
    else:
        body = attend_grad_kernel
        scratch = [
            pltpu.VMEM((frame_size, tokens, 3 * width // frame_size), bf16),
            pltpu.VMEM((frame_size, tokens, width // frame_size), bf16),
        ]
    out = jax.ShapeDtypeStruct(shape, bf16)
    return pl.pallas_call(
        functools.partial(body, blocks=clip_size, count=frame_size),
        grid_spec=pltpu.PrefetchScalarGridSpec(
            num_scalar_prefetch=1,
            grid=(2, rest),
            in_specs=in_specs,
            out_specs=[
                pl.BlockSpec(block, lambda r, j, o: (0, jnp.where(r == 0, j, rest - 1), 0, 0, 0)),
                pl.BlockSpec(block, lambda r, j, o: (0, jnp.where(r == 0, 0, j), 0, 0, 0)),
            ],
            scratch_shapes=scratch,
        ),
        out_shape=[out, out],
        compiler_params=PARAMS,
        cost_estimate=pl.CostEstimate(
            flops=8 * units * tokens * width * width, bytes_accessed=2**24, transcendentals=0
        ),
    )(order.astype(jnp.int32), *arrays)


def pick(value, index, axis):
    return lax.dynamic_index_in_dim(value, index, axis, keepdims=False)


def reduce_blocks(send, keep):
    clip = lax.axis_index("clip")
    across, along = clip % 2, clip // 2
    along_size = lax.axis_size("clip") // 2
    units, rest, blocks, high, width = keep.shape
    total = narrow(wide(keep) + wide(xor_permute(send, "frame", 1)))
    total = total.reshape(units, rest, along_size, 2, high, width)
    if units == 2:
        one, two = total[0], total[1]
    else:
        one, two = total[0, ..., : high // 2, :], total[0, ..., high // 2 :, :]

    def over_rest(value):
        result = wide(value[0])
        for j in range(1, rest):
            result = result + wide(xor_permute(value[j], "frame", 2 * j))
        return narrow(result)

    def over_across(value, axis):
        arrived = xor_permute(pick(value, 1 - across, axis), "clip", 1)
        return narrow(wide(pick(value, across, axis)) + wide(arrived))

    one = over_across(over_rest(one), 1)
    two = over_rest(over_across(two, 2))
    total = jnp.stack((one, two))
    result = wide(pick(total, along, 1))
    for j in range(1, along_size):
        result = result + wide(xor_permute(pick(total, along ^ j, 1), "clip", 2 * j))
    return result


def flips():
    frame_flips = [("frame", 1 << b) for b in range(lax.axis_size("frame").bit_length() - 1)]
    clip_flips = [("clip", 1 << b) for b in range(lax.axis_size("clip").bit_length() - 1)]
    return frame_flips + clip_flips


def sum_everywhere(*parts):
    flat = jnp.concatenate(parts, axis=0)
    for axis, flip in flips():
        flat = flat + xor_permute(flat, axis, flip)
    return flat


def gather_everywhere(rows):
    for axis, flip in flips():
        rows = jnp.concatenate((rows, xor_permute(rows, axis, flip)), axis=0)
    return rows


def tube_order(value):
    blocks = GRID // TUBE_W
    shaped = value.reshape(value.shape[:2] + (blocks, TUBE_W, blocks, TUBE_W) + value.shape[3:])
    return jnp.swapaxes(shaped, 3, 4).reshape(value.shape)


def frame_order(value):
    blocks = GRID // TUBE_W
    shaped = value.reshape(value.shape[:2] + (blocks, blocks, TUBE_W, TUBE_W) + value.shape[3:])
    return jnp.swapaxes(shaped, 3, 4).reshape(value.shape)


def to_tubes(value, clips):
    shaped = value.reshape(clips, TUBES, 1, TUBE_W * TUBE_W, value.shape[-1])
    arrived = lax.all_to_all(shaped, "frame", split_axis=1, concat_axis=2, tiled=True)
    return arrived.reshape(value.shape)


def to_frames(value, clips):
    size = lax.axis_size("frame")
    shaped = value.reshape(clips, TUBES // size, size, TUBE_W * TUBE_W, value.shape[-1])
    returned = lax.all_to_all(shaped, "frame", split_axis=2, concat_axis=1, tiled=True)
    return returned.reshape(value.shape)


def local(
    patches,
    mask_ids,
    action_ids,
    action_table,
    action_proj,
    mask_embed,
    norm_gain,
    norm_bias,
    w_qkv,
    qv_bias,
    w_out,
    out_bias,
    w_fc1,
    fc1_bias,
    w_fc2,
    fc2_bias,
    cotangent,
):
    actions, width = action_table.shape
    clips, frames, tokens_frame, _ = patches.shape
    tokens = clips * frames * tokens_frame
    hidden_width = w_fc1.shape[2]
    frame_size, clip_size = lax.axis_size("frame"), lax.axis_size("clip")
    tube_group = frame_size * frames * TUBE_W * TUBE_W
    onehot = narrow(action_ids.reshape(-1, 1) == jnp.arange(actions, dtype=jnp.int32))
    chosen = dot(onehot, action_table)
    drive = dot(narrow(chosen), action_proj)
    patches = tube_order(patches).reshape(tokens, width)
    mask = tube_order(mask_ids).reshape(tokens, 1)
    cotangent = tube_order(cotangent).reshape(tokens, width)

    gains = norm_gain.reshape(-1, 1, width)
    biases = norm_bias.reshape(-1, 1, width)
    out_biases = out_bias.reshape(-1, 1, width)
    fc2_biases = fc2_bias.reshape(-1, 1, width)
    fc1_biases = fc1_bias.reshape(-1, 1, hidden_width)

    def norm(layer, place):
        spec = vector_spec(2 * layer + place, width)
        return [(gains, spec), (biases, spec)]

    def layer_weights(layer):
        fc1 = (w_fc1, pl.BlockSpec((1, width, width), lambda i: (layer, 0, i)))
        fc1_shift = (fc1_biases, pl.BlockSpec((1, 1, width), lambda i: (layer, 0, i)))
        fc2 = (w_fc2, pl.BlockSpec((1, width, width), lambda i: (layer, i, 0)))
        out = (w_out, pl.BlockSpec((1, width, width), lambda i: (layer, 0, 0)))
        return fc1, fc1_shift, fc2, out

    chunk = pl.BlockSpec((tokens, width), lambda i: (0, i))
    steps = hidden_width // width
    plain_low = ((tokens, width), bf16, None)
    plain = ((tokens, width), f32, None)
    wide_low = ((tokens, hidden_width), bf16, chunk)
    small_out = ((8, width), f32, None)
    matrix = tokens * width * hidden_width
    held = pltpu.VMEM((tokens, width), f32)

    stream_zero, hidden_zero, q_zero, k_zero, v_zero, mixed_zero = project_attend(
        w_qkv,
        qv_bias,
        0,
        tokens_frame,
        start=(patches, mask, mask_embed.reshape(1, width), drive, norm(0, 0)),
        tokens_frame=tokens_frame,
    )
    fc1, fc1_shift, fc2, out = layer_weights(0)
    middle_zero, hidden_two_zero, before_zero, activated_zero, stream_one, hidden_one = call(
        mlp_kernel,
        (steps,),
        [(stream_zero, None), (mixed_zero, None), out, (out_biases, vector_spec(0, width))]
        + norm(0, 1)
        + [fc1, fc1_shift, fc2, (fc2_biases, vector_spec(0, width))]
        + norm(1, 0),
        [plain, plain_low, ((tokens, hidden_width), f32, chunk), wide_low, plain, plain_low],
        flops=5 * matrix,
    )

    tubes_one = to_tubes(hidden_one, clips)
    q_one, k_one, v_one, mixed_tubes = project_attend(w_qkv, qv_bias, 1, tube_group, hidden=tubes_one)
    mixed_one = to_frames(mixed_tubes, clips)
    fc1, fc1_shift, fc2, out = layer_weights(1)
    output, hidden_two_one, activated_one, gu_one, gmid_one, gb_one, go_one, small_one = call(
        mlp_both_kernel,
        (steps,),
        [(stream_one, None), (mixed_one, None), out, (out_biases, vector_spec(1, width))]
        + norm(1, 1)
        + [fc1, fc1_shift, fc2, (fc2_biases, vector_spec(1, width)), (cotangent, None)],
        [plain_low, plain_low, wide_low, wide_low, plain, plain_low, plain_low, small_out],
        [held, held, held],
        flops=10 * matrix,
    )

    mlp_one = reduce_blocks(*gradient_blocks(True, hidden_two_one, gu_one, activated_one, cotangent))
    dq, dk, dv, shifts_one, grouped = project_back(
        to_tubes(go_one, clips), q_one, k_one, v_one, w_qkv, 1, tube_group
    )
    grad_hidden = to_frames(grouped, clips)
    attend_one = reduce_blocks(
        *gradient_blocks(False, tubes_one, dq, dk, dv, mixed_one, gb_one)
    )

    fc1, fc1_shift, fc2, out = layer_weights(0)
    gm_zero, gu_zero, gmid_zero, gb_zero, go_zero, small_zero, small_next = call(
        mlp_back_kernel,
        (steps,),
        [(gmid_one, None), (grad_hidden, None), (stream_one, None), norm(1, 0)[0]]
        + [(middle_zero, None), norm(0, 1)[0], (before_zero, chunk), fc1, fc2, out],
        [plain_low, wide_low, plain, plain_low, plain_low, small_out, small_out],
        [held, held],
        flops=5 * matrix,
    )
    mlp_zero = reduce_blocks(*gradient_blocks(True, hidden_two_zero, gu_zero, activated_zero, gm_zero))
    dq, dk, dv, shifts_zero, patch_grad, small_first = project_back(
        go_zero,
        q_zero,
        k_zero,
        v_zero,
        w_qkv,
        0,
        tokens_frame,
        extra=[norm(0, 0)[0], (stream_zero, None), (gmid_zero, None), (mask, None)],
        tokens_frame=tokens_frame,
    )
    attend_zero = reduce_blocks(*gradient_blocks(False, hidden_zero, dq, dk, dv, mixed_zero, gb_zero))

    gathered = gather_everywhere(
        jnp.concatenate(
            (
                small_first[3 : 3 + clips * frames],
                jnp.broadcast_to(wide(action_ids).reshape(-1, 1), (action_ids.size, 128)),
            ),
            axis=1,
        )
    )
    drive_all = gathered[:, :width]
    ids_all = gathered[:, width].astype(jnp.int32)
    clip, frame = lax.axis_index("clip"), lax.axis_index("frame")
    row_count, column_count = width // clip_size, width // frame_size
    act_count = actions // clip_size
    onehot_all = wide(ids_all[:, None] == jnp.arange(actions, dtype=jnp.int32))
    table_rows = wide(lax.dynamic_slice_in_dim(action_table, clip * row_count, row_count, 1))
    proj_sum = lax.dot_general(
        jnp.dot(onehot_all, table_rows, precision=highest),
        lax.dynamic_slice_in_dim(drive_all, frame * column_count, column_count, 1),
        (((0,), (0,)), ((), ())),
        precision=highest,
    )
    chosen_grad = lax.dot_general(
        drive_all,
        wide(lax.dynamic_slice_in_dim(action_proj, frame * column_count, column_count, 0)),
        (((1,), (1,)), ((), ())),
        precision=highest,
    )
    table_sum = lax.dot_general(
        lax.dynamic_slice_in_dim(onehot_all, clip * act_count, act_count, 1),
        chosen_grad,
        (((0,), (0,)), ((), ())),
        precision=highest,
    )

    def attend_parts(value):
        value = jnp.concatenate((value[0], value[1]), axis=0)
        return value[:, : 3 * column_count], value[:, 3 * column_count :]

    def mlp_parts(value):
        pieces = [value[1][:, i * column_count : (i + 1) * column_count] for i in range(steps)]
        return value[0], jnp.concatenate(pieces, axis=0)

    (qkv_a, out_a), (qkv_b, out_b) = attend_parts(attend_zero), attend_parts(attend_one)
    (fc1_a, fc2_a), (fc1_b, fc2_b) = mlp_parts(mlp_zero), mlp_parts(mlp_one)

    upper = sum_everywhere(small_one, shifts_one)
    lower = sum_everywhere(small_zero, small_next, shifts_zero, small_first)

    def rows(*values):
        return jnp.concatenate([v.reshape(1, -1) for v in values], axis=0)

    norm_shape = (2, 2, width)
    gain_grad = rows(lower[24], lower[0], lower[8], upper[0]).reshape(norm_shape)
    bias_grad = rows(lower[25], lower[1], lower[9], upper[1]).reshape(norm_shape)
    shape = (clips, frames, tokens_frame, width)
    return (
        frame_order(output.reshape(shape)),
        frame_order(patch_grad.reshape(shape)),
        table_sum,
        proj_sum,
        lower[26],
        gain_grad,
        bias_grad,
        jnp.stack((qkv_a, qkv_b)),
        jnp.concatenate((lower[16:18], upper[8:10])).reshape(norm_shape),
        jnp.stack((out_a, out_b)),
        rows(lower[2], upper[2]),
        jnp.stack((fc1_a, fc1_b)),
        rows(lower[4 : 4 + steps], upper[4 : 4 + steps]),
        jnp.stack((fc2_a, fc2_b)),
        rows(lower[3], upper[3]),
    )


def solution(mesh):
    rows = P("clip", "frame", None, None)
    blocks = P(None, "clip", "frame")
    in_specs = (rows, P("clip", "frame", None), P("clip", "frame")) + (P(),) * 13 + (rows,)
    out_specs = (
        rows, rows, P("clip", "frame"), P("clip", "frame"), P(), P(), P(),
        blocks, P(), blocks, P(), blocks, P(), blocks, P(),
    )
    return jax.shard_map(local, mesh=mesh, in_specs=in_specs, out_specs=out_specs, check_vma=False)
```

time: 1270 us -> 493 us (0.39)
  waiting for transfers between devices: 847 us -> 132 us
  Pallas kernels: 0 us -> 189 us
  matrix products: 151 us -> 5.41 us
  local copies, waits for them, and re-layouts: 134 us -> 40.6 us
  starting transfers between devices: 8.31 us -> 73.7 us
  other arithmetic: 69.8 us -> 26 us
  between operations: 16.6 us -> 2.09 us
  blocking collectives: 29.9 us -> 15.7 us
    reduce_scatter x7 -> x0, waiting for transfers between devices: 602 us -> none  [the longest x1 159 us: local(): lax.psum_scatter(jnp.stack((large_one[2], large_two[2])).astype(jnp.bfloa...]
    pallas_call x0 -> x11, Pallas kernels: none -> 189 us  [the longest x7 136 us: call(): pl.pallas_call(body, grid=grid, in_specs=[s or whole_spec(a.shape) for a,...]
    dot_general x41 -> x5, matrix products: 151 us -> 5.41 us  [the longest x1 1.36 us: local(): lax.dot_general(drive_all, wide(lax.dynamic_slice_in_dim(action_proj, fra...]
    psum x1 -> x0, waiting for transfers between devices: 130 us -> none  [local(): lax.psum((jnp.stack((small_one[0], small_two[0])), jnp.stack((small_one[1...]
    ppermute x0 -> x47, waiting for transfers between devices: none -> 110 us  [xor_permute(): return lax.ppermute(value, axis, [(i, i ^ flip) for i in range(count)])]
    unnamed x18 -> x0, waiting for transfers between devices: 94.4 us -> none
    ppermute x0 -> x47, starting transfers between devices: none -> 62 us  [xor_permute(): return lax.ppermute(value, axis, [(i, i ^ flip) for i in range(count)])]
    convert_element_type x18 -> x0, local copies, waits for them, and re-layouts: 42.7 us -> none  [the longest x3 8.85 us: block_backward(): key_grad.astype(jnp.bfloat16)]
  transfers between devices with their start and end apart: 15 -> 50, of which waited for: 13 -> 28; matrix products, arithmetic and copies ran while one was open for 10% -> 10% of each run, Pallas kernels for 0% -> 19%
where the time goes in v1:
time: 493 us; the launch traced here: 484 us
  Pallas kernels  189 us (38%)
  waiting for transfers between devices  132 us (27%)
  starting transfers between devices  73.7 us (15%)
  local copies, waits for them, and re-layouts  40.6 us (8%)
  other arithmetic  26 us (5%)
  blocking collectives  15.7 us (3%)
  matrix products  5.41 us (1%)
    pallas_call x7, Pallas kernels, call(): pl.pallas_call(body, grid=grid, in_specs=[s or whole_spec(a.shape) for a,...  136 us
    ppermute x47, waiting for transfers between devices, xor_permute(): return lax.ppermute(value, axis, [(i, i ^ flip) for i in range(count)])  110 us
    ppermute x47, starting transfers between devices, xor_permute(): return lax.ppermute(value, axis, [(i, i ^ flip) for i in range(count)])  62 us
    pallas_call x4, Pallas kernels, gradient_blocks(): pl.pallas_call(functools.partial(body, blocks=clip_size, count=frame_size...  52.8 us
    all_to_all x1, blocking collectives, to_tubes(): lax.all_to_all(shaped, 'frame', split_axis=1, concat_axis=2, tiled=True)  15.7 us
    convert_element_type x12, other arithmetic, narrow(): return value.astype(bf16)  14.7 us
    all_to_all x1, waiting for transfers between devices, to_tubes(): lax.all_to_all(shaped, 'frame', split_axis=1, concat_axis=2, tiled=True)  11.6 us
    all_to_all x2, waiting for transfers between devices, to_frames(): lax.all_to_all(shaped, 'frame', split_axis=2, concat_axis=1, tiled=True)  10 us
  transfers between devices with their start and end apart: 50, of which 28 were waited for; matrix products, arithmetic and copies ran while one was open for 10% of the time, Pallas kernels for 19%

profile of v1, /device:TPU:0, one launch (start us, length us, event | category | flops | bytes accessed | tf_op | source)
XLA Modules:
  0.0 484.2 jit_solution(9016594712490535781)
XLA Ops:
  0.7 1.8 reshape.190
  10.3 11.1 %shard_map.280 = (f32[512,768]{1,0:T(8,128)}, bf16[512,768]{1,0:T(8,128)(2,1)}, bf16[512,768]{1,0:T(8,128)(2,1)}, bf16[512,768]{1,0:T(8,128)(2,1)}, bf16[512,768]{1,0:T(8,128)(2,1)}, /*index=5*/bf16[512,768]{1,0:T(8,128)(2,1)}) custom-call(bf16[512,768]{1,0:T(8,128)(2,1)} %reshape_reshape.15.refs_0_, s32[512,1]{1,0:T(8,128)} %reshape_reshape.20.refs_1_.refs_10_, ...), custom_call_target="tpu_custom_call" | custom-call | flops 2415919104 | bytes 11040256 | tf_op jit(solution)/shard_map/pallas_call | solution.py:291
  21.4 15.0 %shard_map.281 = (f32[512,768]{1,0:T(8,128)}, bf16[512,768]{1,0:T(8,128)(2,1)}, f32[512,3072]{1,0:T(8,128)}, bf16[512,3072]{1,0:T(8,128)(2,1)}, f32[512,768]{1,0:T(8,128)}, /*index=5*/bf16[512,768]{1,0:T(8,128)(2,1)}) custom-call(f32[512,768]{1,0:T(8,128)} %get-tuple-element.65.stream.refs_8_, bf16[512,768]{1,0:T(8,128)(2,1)} %get-tuple-element.66.mixed, ...), custom_call_target="tpu_custom_call" | custom-call | flops 6039797760 | bytes 11839488 | tf_op jit(solution)/shard_map/pallas_call | solution.py:291
  37.7 15.7 %all_to_all.60 = bf16[2,16,1,16,768]{4,3,0,2,1:T(8,128)(2,1)S(1)} all-to-all(bf16[2,16,1,16,768]{4,3,0,2,1:T(8,128)(2,1)S(1)} %copy.83), channel_id=1, replica_groups=mesh['clip'=8,'frame'=4] {'frame'}, dimensions={1} | all-to-all | bytes 1572864 | tf_op jit(solution)/shard_map/all_to_all | solution.py:547
  54.4 19.5 %shard_map.282 = (bf16[512,768]{1,0:T(8,128)(2,1)}, bf16[512,768]{1,0:T(8,128)(2,1)}, bf16[512,768]{1,0:T(8,128)(2,1)}, bf16[512,768]{1,0:T(8,128)(2,1)}) custom-call(bf16[512,768]{1,0:T(8,128)(2,1)} %bitcast.268, bf16[2,768,2304]{2,1,0:T(8,128)(2,1)} %refs_6_.5, bf16[2,768,2304]{2,1,0:T(8,128)(2,1)} %refs_6_.5, bf16[2,768,2304]{2,1,0:T(8,128)(2,1)} %refs_6_.5, ...), custom_call_target="tpu_custom_call" | custom-call | flops 2415919104 | bytes 11022336 | tf_op jit(solution)/shard_map/pallas_call | solution.py:291
  73.9 2.1 copy.86
  76.0 3.8 all-to-all-start.1
  81.4 10.0 %all-to-all-done.1 = bf16[2,4,4,16,768]{4,3,1,0,2:T(8,128)(2,1)S(1)} async-done(((bf16[2,4,4,16,768]{4,3,1,0,2:T(8,128)(2,1)}), bf16[2,4,4,16,768]{4,3,1,0,2:T(8,128)(2,1)S(1)}, u32[]{:S(2)}, u32[]{:S(2)}) %all-to-all-start.1) | async-done | bytes 786464 | tf_op jit(solution)/shard_map/all_to_all | solution.py:554
  92.4 22.0 %shard_map.283 = (bf16[512,768]{1,0:T(8,128)(2,1)}, bf16[512,768]{1,0:T(8,128)(2,1)}, bf16[512,3072]{1,0:T(8,128)(2,1)}, bf16[512,3072]{1,0:T(8,128)(2,1)}, f32[...) custom-call(f32[512,768]{1,0:T(8,128)} %get-tuple-element.67.stream.stream_next, ...), custom_call_target="tpu_custom_call" | custom-call | flops 12079595520 | bytes 12220416 | tf_op jit(solution)/shard_map/pallas_call | solution.py:291
  114.4 2.1 copy.90
  116.6 3.9 all-to-all-start.2
  120.5 11.6 %all-to-all-done.2 = bf16[2,16,1,16,768]{4,3,0,2,1:T(8,128)(2,1)S(1)} async-done(((bf16[2,16,1,16,768]{4,3,0,2,1:T(8,128)(2,1)}), bf16[2,16,1,16,768]{4,3,0,2,1:T(8,128)(2,1)S(1)}, u32[]{:S(2)}, u32[]{:S(2)}) %all-to-all-start.2) | async-done | bytes 786464 | tf_op jit(solution)/shard_map/all_to_all | solution.py:547
  133.0 27.7 %shard_map.284 = (bf16[512,768]{1,0:T(8,128)(2,1)}, bf16[512,768]{1,0:T(8,128)(2,1)}, bf16[512,768]{1,0:T(8,128)(2,1)}, f32[8,768]{1,0:T(8,128)}, bf16[512,768]{1,0:T(8,128)(2,1)}) custom-call(bf16[512,768]{1,0:T(8,128)(2,1)} %bitcast.270, bf16[512,768]{1,0:T(8,128)(2,1)} %get-tuple-element.73.refs_1_, bf16[512,768]{1,0:T(8,128)(2,1)} %get-tuple-element.74.refs_2_, ...), custom_call_target="tpu_custom_call" | custom-call | flops 3019898880 | bytes 12189696 | tf_op jit(solution)/shard_map/pallas_call | solution.py:291
  163.2 3.7 collective-permute-done.11
  169.0 2.0 collective-permute-done.12
  172.7 16.2 %shard_map.290 = (bf16[2,2,8,96,768]{4,3,2,1,0:T(8,128)(2,1)}, bf16[2,2,8,96,768]{4,3,2,1,0:T(8,128)(2,1)}) custom-call(s32[4]{0:T(128)} %pad_add_fusion.order, bf16[512,768]{1,0:T(8,128)(2,1)} %get-tuple-element.110.hidden_two, bf16[512,3072]{1,0:T(8,128)(2,1)} %get-tuple-element.111.gu, bf16[512,3072]{1,0:T(8,128)(2,1)} %get-tuple-element.112.activated, ...), custom_call_target="tpu_custom_call" | custom-call | flops 4831838208 | bytes 16777216 | tf_op jit(solution)/shard_map/pallas_call | solution.py:459
  191.6 4.0 all-to-all-start.3
  195.6 2.7 collective-permute-start.14
  198.2 10.1 %shard_map.288 = (bf16[1,2,8,96,768]{4,3,2,1,0:T(8,128)(2,1)}, bf16[1,2,8,96,768]{4,3,2,1,0:T(8,128)(2,1)}) custom-call(s32[4]{0:T(128)} %pad_add_fusion.order, bf16[512,768]{1,0:T(8,128)(2,1)} %bitcast.269, bf16[512,768]{1,0:T(8,128)(2,1)} %get-tuple-element.98.dq, bf16[512,768]{1,0:T(8,128)(2,1)} %get-tuple-element.99.dk, ...), custom_call_target="tpu_custom_call" | custom-call | flops 2415919104 | bytes 16777216 | tf_op jit(solution)/shard_map/pallas_call | solution.py:459
  210.8 18.8 %shard_map.285 = (bf16[512,768]{1,0:T(8,128)(2,1)}, bf16[512,3072]{1,0:T(8,128)(2,1)}, f32[512,768]{1,0:T(8,128)}, bf16[512,768]{1,0:T(8,128)(2,1)}, bf16[512,76...) custom-call(f32[512,768]{1,0:T(8,128)} %get-tuple-element.71.gmid_next, bf16[512,768]{1,0:T(8,128)(2,1)} %bitcast.279, ...), custom_call_target="tpu_custom_call" | custom-call | flops 6039797760 | bytes 16527360 | tf_op jit(solution)/shard_map/pallas_call | solution.py:291
  229.6 22.1 %shard_map.286 = (bf16[512,768]{1,0:T(8,128)(2,1)}, bf16[512,768]{1,0:T(8,128)(2,1)}, bf16[512,768]{1,0:T(8,128)(2,1)}, f32[8,768]{1,0:T(8,128)}, bf16[512,768]{1,0:T(8,128)(2,1)}, /*index=5*/f32[8,768]{1,0:T(8,128)}) custom-call(bf16[512,768]{1,0:T(8,128)(2,1)} %get-tuple-element.79.refs_0_, bf16[512,768]{1,0:T(8,128)(2,1)} %get-tuple-element.80.refs_1_, ...), custom_call_target="tpu_custom_call" | custom-call | flops 3019898880 | bytes 13769728 | tf_op jit(solution)/shard_map/pallas_call | solution.py:291
  253.7 2.0 collective-permute-start.1
  262.0 16.1 %shard_map.289 = (bf16[2,2,8,96,768]{4,3,2,1,0:T(8,128)(2,1)}, bf16[2,2,8,96,768]{4,3,2,1,0:T(8,128)(2,1)}) custom-call(s32[4]{0:T(128)} %pad_add_fusion.order, bf16[512,768]{1,0:T(8,128)(2,1)} %get-tuple-element.104.hidden_two, bf16[512,3072]{1,0:T(8,128)(2,1)} %get-tuple-element.105.gu, bf16[512,3072]{1,0:T(8,128)(2,1)} %get-tuple-element.106.activated, ...), custom_call_target="tpu_custom_call" | custom-call | flops 4831838208 | bytes 16777216 | tf_op jit(solution)/shard_map/pallas_call | solution.py:459
  278.1 2.0 collective-permute-start.6
  280.5 10.4 %shard_map.287 = (bf16[1,2,8,96,768]{4,3,2,1,0:T(8,128)(2,1)}, bf16[1,2,8,96,768]{4,3,2,1,0:T(8,128)(2,1)}) custom-call(s32[4]{0:T(128)} %pad_add_fusion.order, bf16[512,768]{1,0:T(8,128)(2,1)} %get-tuple-element.91.hidden, bf16[512,768]{1,0:T(8,128)(2,1)} %get-tuple-element.92.dq, bf16[512,768]{1,0:T(8,128)(2,1)} %get-tuple-element.93.dk, ...), custom_call_target="tpu_custom_call" | custom-call | flops 2415919104 | bytes 16777216 | tf_op jit(solution)/shard_map/pallas_call | solution.py:459
  295.1 2.5 concatenate.63
  305.8 3.0 collective-permute-done.8
  308.7 2.7 collective-permute-start.9
  312.3 2.0 collective-permute-done.9
  320.8 2.3 add_convert_fusion.2
  325.6 10.4 %collective-permute-done.24 = bf16[4,2,48,768]{3,2,0,1:T(8,128)(2,1)S(1)} collective-permute-done((bf16[4,2,48,768]{3,2,0,1:T(8,128)(2,1)S(1)}, bf16[4,2,48,768]{3,2,0,1:T(8,128)(2,1)S(1)}, u32[]{:S(2)}, u32[]{:S(2)}) %collective-permute-start.24) | collective-permute-done | bytes 589856 | tf_op jit(solution)/shard_map/ppermute | solution.py:359
  336.8 1.8 collective-permute-done.26
  338.8 3.0 collective-permute-start.27
  341.8 2.4 add_convert_fusion.3
  344.3 2.2 collective-permute-done.27
  346.7 4.6 collective-permute-start.30
  352.6 2.7 collective-permute-done.30
  355.4 3.2 collective-permute-done.29
  358.6 2.0 collective-permute-start.16
  361.5 2.1 collective-permute-start.19
  363.6 6.1 %collective-permute-done.16 = bf16[4,2,48,768]{3,2,0,1:T(8,128)(2,1)S(1)} collective-permute-done((bf16[4,2,48,768]{3,2,0,1:T(8,128)(2,1)S(1)}, bf16[4,2,48,768]{3,2,0,1:T(8,128)(2,1)S(1)}, u32[]{:S(2)}, u32[]{:S(2)}) %collective-permute-start.16) | collective-permute-done | bytes 589856 | tf_op jit(solution)/shard_map/ppermute | solution.py:359
  369.9 1.8 collective-permute-start.17
  371.7 2.3 collective-permute-done.19
  374.1 4.1 add_convert_fusion
  378.4 2.1 collective-permute-start.40
  380.6 2.9 collective-permute-start.22
  385.1 2.6 collective-permute-done.22
  387.7 3.1 collective-permute-done.21
  391.2 1.7 collective-permute-start.42
  392.9 5.4 %collective-permute-done.40 = bf16[4,2,96,768]{3,2,1,0:T(8,128)(2,1)S(1)} collective-permute-done((bf16[4,2,96,768]{3,2,1,0:T(8,128)(2,1)S(1)}, bf16[4,2,96,768]{3,2,1,0:T(8,128)(2,1)S(1)}, u32[]{:S(2)}, u32[]{:S(2)}) %collective-permute-start.40) | collective-permute-done | bytes 1179680 | tf_op jit(solution)/shard_map/ppermute | solution.py:359
  398.6 3.2 collective-permute-start.41
  401.8 4.1 add_convert_fusion.1
  406.1 1.8 collective-permute-start.32
  407.9 12.2 %collective-permute-done.42 = bf16[2,4,96,768]{3,2,1,0:T(8,128)(2,1)S(1)} collective-permute-done((bf16[2,4,96,768]{3,2,1,0:T(8,128)(2,1)S(1)}, bf16[2,4,96,768]{3,2,1,0:T(8,128)(2,1)S(1)}, u32[]{:S(2)}, u32[]{:S(2)}) %collective-permute-start.42) | collective-permute-done | bytes 1179680 | tf_op jit(solution)/shard_map/ppermute | solution.py:359
  421.6 1.7 collective-permute-start.34
  423.6 9.2 %collective-permute-done.41 = bf16[4,96,768]{2,1,0:T(8,128)(2,1)} collective-permute-done((bf16[4,96,768]{2,1,0:T(8,128)(2,1)S(1)}, bf16[4,96,768]{2,1,0:T(8,128)(2,1)}, u32[]{:S(2)}, u32[]{:S(2)}) %collective-permute-start.41) | collective-permute-done | bytes 589856 | tf_op jit(solution)/shard_map/ppermute | solution.py:359
  434.1 2.0 collective-permute-done.43
  436.3 3.6 collective-permute-start.46
  441.1 1.8 collective-permute-start.33
  443.0 9.8 %collective-permute-done.34 = bf16[2,4,96,768]{3,2,1,0:T(8,128)(2,1)S(1)} collective-permute-done((bf16[2,4,96,768]{3,2,1,0:T(8,128)(2,1)S(1)}, bf16[2,4,96,768]{3,2,1,0:T(8,128)(2,1)S(1)}, u32[]{:S(2)}, u32[]{:S(2)}) %collective-permute-start.34) | collective-permute-done | bytes 1179680 | tf_op jit(solution)/shard_map/ppermute | solution.py:359
  455.0 9.5 %collective-permute-done.45 = bf16[2,96,768]{2,1,0:T(8,128)(2,1)S(1)} collective-permute-done((bf16[2,96,768]{2,1,0:T(8,128)(2,1)S(1)}, bf16[2,96,768]{2,1,0:T(8,128)(2,1)S(1)}, u32[]{:S(2)}, u32[]{:S(2)}) %collective-permute-start.45) | collective-permute-done | bytes 294944 | tf_op jit(solution)/shard_map/ppermute | solution.py:359
  466.1 3.5 collective-permute-start.36
  469.7 4.2 collective-permute-done.38
  473.9 7.5 %collective-permute-done.37 = bf16[2,96,768]{2,1,0:T(8,128)(2,1)S(1)} collective-permute-done((bf16[2,96,768]{2,1,0:T(8,128)(2,1)S(1)}, bf16[2,96,768]{2,1,0:T(8,128)(2,1)S(1)}, u32[]{:S(2)}, u32[]{:S(2)}) %collective-permute-start.37) | collective-permute-done | bytes 294944 | tf_op jit(solution)/shard_map/ppermute | solution.py:359
  (259 shorter events, 72.9 us)
Async XLA Ops:
  0.6 8.6 %copy-start = (bf16[768,768]{1,0:T(8,128)(2,1)S(1)}, bf16[768,768]{1,0:T(8,128)(2,1)}, u32[]{:S(2)}) copy-start(bf16[768,768]{1,0:T(8,128)(2,1)} %param.21) | copy-start | bytes 3538948
  76.0 15.4 %all-to-all-start.1 = ((bf16[2,4,4,16,768]{4,3,1,0,2:T(8,128)(2,1)}), bf16[2,4,4,16,768]{4,3,1,0,2:T(8,128)(2,1)S(1)}, u32[]{:S(2)}, u32[]{:S(2)}) async-start(bf16[2,4,4,16,768]{4,3,1,0,2:T(8,128)(2,1)} %copy.86), calls=%async_computation.1 | async-start | bytes 1572864 | tf_op jit(solution)/shard_map/all_to_all | solution.py:554
  116.6 15.5 %all-to-all-start.2 = ((bf16[2,16,1,16,768]{4,3,0,2,1:T(8,128)(2,1)}), bf16[2,16,1,16,768]{4,3,0,2,1:T(8,128)(2,1)S(1)}, u32[]{:S(2)}, u32[]{:S(2)}) async-start(bf16[2,16,1,16,768]{4,3,0,2,1:T(8,128)(2,1)} %copy.90), calls=%async_computation.2 | async-start | bytes 1572864 | tf_op jit(solution)/shard_map/all_to_all | solution.py:547
  161.5 1.2 collective-permute-start.10
  162.7 4.2 collective-permute-start.11
  166.9 4.2 collective-permute-start.12
  171.0 24.5 %collective-permute-start.13 = (f32[16,768]{1,0:T(8,128)S(1)}, f32[16,768]{1,0:T(8,128)S(1)}, u32[]{:S(2)}, u32[]{:S(2)}) collective-permute-start(f32[16,768]{1,0:T(8,128)S(1)} %add.236), channel_id=1, source_target_pairs={{0,8},{4,12},{8,0},{12,4},{16,24},{20,28},{24,16},{28,20},{1,9},{5... | collective-permute-start | bytes 147464 | tf_op jit(solution)/shard_map/ppermute | solution.py:359
  172.7 16.2 %copy-start.4 = (bf16[512,768]{1,0:T(8,128)(2,1)S(1)}, bf16[512,768]{1,0:T(8,128)(2,1)}, u32[]{:S(2)}) copy-start(bf16[512,768]{1,0:T(8,128)(2,1)} %get-tuple-element.70) | copy-start | bytes 2359300
  190.4 183.7 %collective-permute-start.39 = (bf16[2,2,8,96,768]{4,3,2,1,0:T(8,128)(2,1)}, bf16[2,2,8,96,768]{4,3,2,1,0:T(8,128)(2,1)}, u32[]{:S(2)}, u32[]{:S(2)}) collective-permute-start(bf16[2,2,8,96,768]{4,3,2,1,0:T(8,128)(2,1)} %get-tuple-element.114), channel_id=1, source_target_pairs={{0,1},{1,0},{2,3},{3,2},{4,5},{5,4},{6,7},{7,6},{8,9},{9,8},{10,11... | collective-permute-start | bytes 14155784 | tf_op jit(solution)/shard_map/ppermute | solution.py:359
  191.6 18.3 %all-to-all-start.3 = ((bf16[2,4,4,16,768]{4,3,1,0,2:T(8,128)(2,1)}), bf16[2,4,4,16,768]{4,3,1,0,2:T(8,128)(2,1)S(1)}, u32[]{:S(2)}, u32[]{:S(2)}) async-start(bf16[2,4,4,16,768]{4,3,1,0,2:T(8,128)(2,1)} %copy.93), calls=%async_computation.3 | async-start | bytes 1572864 | tf_op jit(solution)/shard_map/all_to_all | solution.py:554
  195.6 13.0 %collective-permute-start.14 = (f32[16,768]{1,0:T(8,128)S(1)}, f32[16,768]{1,0:T(8,128)S(1)}, u32[]{:S(2)}, u32[]{:S(2)}) collective-permute-start(f32[16,768]{1,0:T(8,128)S(1)} %add.237), channel_id=1, source_target_pairs={{0,16},{4,20},{8,24},{12,28},{16,0},{20,4},{24,8},{28,12},{1,17},{... | collective-permute-start | bytes 147464 | tf_op jit(solution)/shard_map/ppermute | solution.py:359
  208.4 112.4 %collective-permute-start.23 = (bf16[1,2,8,96,768]{4,3,2,1,0:T(8,128)(2,1)}, bf16[1,2,8,96,768]{4,3,2,1,0:T(8,128)(2,1)}, u32[]{:S(2)}, u32[]{:S(2)}) collective-permute-start(bf16[1,2,8,96,768]{4,3,2,1,0:T(8,128)(2,1)} %get-tuple-element.103), channel_id=1, source_target_pairs={{0,1},{1,0},{2,3},{3,2},{4,5},{5,4},{6,7},{7,6},{8,9},{9,8},{10,11... | collective-permute-start | bytes 7077896 | tf_op jit(solution)/shard_map/ppermute | solution.py:359
  229.6 23.3 %copy-start.13 = (f32[8,768]{1,0:T(8,128)S(1)}, f32[8,768]{1,0:T(8,128)}, u32[]{:S(2)}) copy-start(f32[8,768]{1,0:T(8,128)} %get-tuple-element.86) | copy-start | bytes 73732
  229.6 23.3 %copy-start.12 = (f32[8,768]{1,0:T(8,128)S(1)}, f32[8,768]{1,0:T(8,128)}, u32[]{:S(2)}) copy-start(f32[8,768]{1,0:T(8,128)} %get-tuple-element.87) | copy-start | bytes 73732
  252.5 1.2 collective-permute-start
  253.7 3.8 collective-permute-start.1
  257.5 3.9 collective-permute-start.2
  259.8 18.3 %collective-permute-start.5 = (f32[32,768]{1,0:T(8,128)S(1)}, f32[32,768]{1,0:T(8,128)S(1)}, u32[]{:S(2)}, u32[]{:S(2)}) collective-permute-start(f32[32,768]{1,0:T(8,128)S(1)} %constant_dynamic-update-slice_fusion), channel_id=1, source_target_pairs={{0,1},{1,0},{2,3},{3,2},{4,5},{5,4},{6,7},{7,6},{8,9},{9,8},{10,11... | collective-permute-start | bytes 294920 | tf_op jit(solution)/shard_map/ppermute | solution.py:359
  261.4 18.6 %collective-permute-start.3 = (f32[16,896]{1,0:T(8,128)S(1)}, f32[16,896]{1,0:T(8,128)S(1)}, u32[]{:S(2)}, u32[]{:S(2)}) collective-permute-start(f32[16,896]{1,0:T(8,128)S(1)} %pad_maximum_fusion.6), channel_id=1, source_target_pairs={{0,8},{4,12},{8,0},{12,4},{16,24},{20,28},{24,16},{28,20},{1,9},{5... | collective-permute-start | bytes 172040 | tf_op jit(solution)/shard_map/ppermute | solution.py:359
  278.1 14.4 %collective-permute-start.6 = (f32[32,768]{1,0:T(8,128)S(1)}, f32[32,768]{1,0:T(8,128)S(1)}, u32[]{:S(2)}, u32[]{:S(2)}) collective-permute-start(f32[32,768]{1,0:T(8,128)S(1)} %add.229), channel_id=1, source_target_pairs={{0,2},{1,3},{2,0},{3,1},{4,6},{5,7},{6,4},{7,5},{8,10},{9,11},{10,... | collective-permute-start | bytes 294920 | tf_op jit(solution)/shard_map/ppermute | solution.py:359
  280.1 13.5 %collective-permute-start.4 = (f32[32,896]{1,0:T(8,128)S(1)}, f32[32,896]{1,0:T(8,128)S(1)}, u32[]{:S(2)}, u32[]{:S(2)}) collective-permute-start(f32[32,896]{1,0:T(8,128)S(1)} %concatenate.62), channel_id=1, source_target_pairs={{0,16},{4,20},{8,24},{12,28},{16,0},{20,4},{24,8},{28,12},{1,17},{... | collective-permute-start | bytes 344072 | tf_op jit(solution)/shard_map/ppermute | solution.py:359
  280.5 10.4 %copy-start.6 = (bf16[512,768]{1,0:T(8,128)(2,1)S(1)}, bf16[512,768]{1,0:T(8,128)(2,1)}, u32[]{:S(2)}) copy-start(bf16[512,768]{1,0:T(8,128)(2,1)} %get-tuple-element.84) | copy-start | bytes 2359300
  292.5 49.3 %collective-permute-start.15 = (bf16[1,2,8,96,768]{4,3,2,1,0:T(8,128)(2,1)}, bf16[1,2,8,96,768]{4,3,2,1,0:T(8,128)(2,1)}, u32[]{:S(2)}, u32[]{:S(2)}) collective-permute-start(bf16[1,2,8,96,768]{4,3,2,1,0:T(8,128)(2,1)} %get-tuple-element.97), channel_id=1, source_target_pairs={{0,1},{1,0},{2,3},{3,2},{4,5},{5,4},{6,7},{7,6},{8,9},{9,8},{10,11... | collective-permute-start | bytes 7077896 | tf_op jit(solution)/shard_map/ppermute | solution.py:359
  292.5 109.4 %collective-permute-start.31 = (bf16[2,2,8,96,768]{4,3,2,1,0:T(8,128)(2,1)}, bf16[2,2,8,96,768]{4,3,2,1,0:T(8,128)(2,1)}, u32[]{:S(2)}, u32[]{:S(2)}) collective-permute-start(bf16[2,2,8,96,768]{4,3,2,1,0:T(8,128)(2,1)} %get-tuple-element.109), channel_id=1, source_target_pairs={{0,1},{1,0},{2,3},{3,2},{4,5},{5,4},{6,7},{7,6},{8,9},{9,8},{10,11... | collective-permute-start | bytes 14155784 | tf_op jit(solution)/shard_map/ppermute | solution.py:359
  293.6 9.4 %collective-permute-start.7 = (f32[32,768]{1,0:T(8,128)}, f32[32,768]{1,0:T(8,128)}, u32[]{:S(2)}, u32[]{:S(2)}) collective-permute-start(f32[32,768]{1,0:T(8,128)} %add.230), channel_id=1, source_target_pairs={{0,4},{4,0},{8,12},{12,8},{16,20},{20,16},{24,28},{28,24},{1,5},{5... | collective-permute-start | bytes 294920 | tf_op jit(solution)/shard_map/ppermute | solution.py:359
  297.6 21.2 %slice-start.4 = ((f32[16,768]{1,0:T(8,128)}), f32[2,768]{1,0:T(2,128)S(1)}, s32[]{:S(2)}) async-start(f32[16,768]{1,0:T(8,128)} %copy-done.9), calls=%async_computation.8 | async-start | bytes 12288 | tf_op jit(solution)/shard_map/slice | solution.py:749
  297.6 23.1 %copy-start.1 = (bf16[1,2,8,96,768]{4,3,2,1,0:T(8,128)(2,1)S(1)}, bf16[1,2,8,96,768]{4,3,2,1,0:T(8,128)(2,1)}, u32[]{:S(2)}) copy-start(bf16[1,2,8,96,768]{4,3,2,1,0:T(8,128)(2,1)} %get-tuple-element.102) | copy-start | bytes 7077892
  304.0 4.7 collective-permute-start.8
  308.7 5.6 %collective-permute-start.9 = (f32[32,768]{1,0:T(8,128)S(1)}, f32[32,768]{1,0:T(8,128)S(1)}, u32[]{:S(2)}, u32[]{:S(2)}) collective-permute-start(f32[32,768]{1,0:T(8,128)S(1)} %add.232), channel_id=1, source_target_pairs={{0,16},{4,20},{8,24},{12,28},{16,0},{20,4},{24,8},{28,12},{1,17},{... | collective-permute-start | bytes 294920 | tf_op jit(solution)/shard_map/ppermute | solution.py:359
  323.3 12.7 %collective-permute-start.24 = (bf16[4,2,48,768]{3,2,0,1:T(8,128)(2,1)S(1)}, bf16[4,2,48,768]{3,2,0,1:T(8,128)(2,1)S(1)}, u32[]{:S(2)}, u32[]{:S(2)}) collective-permute-start(bf16[4,2,48,768]{3,2,0,1:T(8,128)(2,1)S(1)} %bitcast.289), channel_id=1, source_target_pairs={{0,2},{1,3},{2,0},{3,1},{4,6},{5,7},{6,4},{7,5},{8,10},{9,11},{10,... | collective-permute-start | bytes 1769480 | tf_op jit(solution)/shard_map/ppermute | solution.py:359
  324.3 14.3 %collective-permute-start.26 = (bf16[2,4,48,768]{3,2,1,0:T(8,128)(2,1)S(1)}, bf16[2,4,48,768]{3,2,1,0:T(8,128)(2,1)S(1)}, u32[]{:S(2)}, u32[]{:S(2)}) collective-permute-start(bf16[2,4,48,768]{3,2,1,0:T(8,128)(2,1)S(1)} %dynamic-slice_bitcast_fusion.4), channel_id=1, source_target_pairs={{0,4},{4,0},{8,12},{12,8},{16,20},{20,16},{24,28},{28,24},{1,5},{5... | collective-permute-start | bytes 1769480 | tf_op jit(solution)/shard_map/ppermute | solution.py:359
  336.2 10.4 %collective-permute-start.25 = (bf16[4,48,768]{2,1,0:T(8,128)(2,1)S(1)}, bf16[4,48,768]{2,1,0:T(8,128)(2,1)S(1)}, u32[]{:S(2)}, u32[]{:S(2)}) collective-permute-start(bf16[4,48,768]{2,1,0:T(8,128)(2,1)S(1)} %dynamic-slice_bitcast_fusion.6), channel_id=1, source_target_pairs={{0,4},{4,0},{8,12},{12,8},{16,20},{20,16},{24,28},{28,24},{1,5},{5... | collective-permute-start | bytes 884744 | tf_op jit(solution)/shard_map/ppermute | solution.py:359
  338.8 7.7 %collective-permute-start.27 = (bf16[4,48,768]{2,1,0:T(8,128)(2,1)S(1)}, bf16[4,48,768]{2,1,0:T(8,128)(2,1)S(1)}, u32[]{:S(2)}, u32[]{:S(2)}) collective-permute-start(bf16[4,48,768]{2,1,0:T(8,128)(2,1)S(1)} %slice_bitcast_fusion.6), channel_id=1, source_target_pairs={{0,2},{1,3},{2,0},{3,1},{4,6},{5,7},{6,4},{7,5},{8,10},{9,11},{10,... | collective-permute-start | bytes 884744 | tf_op jit(solution)/shard_map/ppermute | solution.py:359
  344.2 7.8 %copy-start.15 = (f32[1,768]{1,0:T(1,128)S(1)}, f32[1,768]{1,0:T(1,128)}, u32[]{:S(2)}) copy-start(f32[1,768]{1,0:T(1,128)} %get-tuple-element.196) | copy-start | bytes 9220
  344.2 7.8 %copy-start.16 = (f32[1,768]{1,0:T(1,128)S(1)}, f32[1,768]{1,0:T(1,128)}, u32[]{:S(2)}) copy-start(f32[1,768]{1,0:T(1,128)} %get-tuple-element.197) | copy-start | bytes 9220
  344.2 7.8 %copy-start.17 = (f32[1,768]{1,0:T(1,128)S(1)}, f32[1,768]{1,0:T(1,128)}, u32[]{:S(2)}) copy-start(f32[1,768]{1,0:T(1,128)} %get-tuple-element.205) | copy-start | bytes 9220
  346.5 27.6 %slice-start = ((s8[4718592]{0:T(1024)(128)(4,1)}), s8[4194304]{0:T(1024)(128)(4,1)S(1)}, s32[]{:S(2)}) async-start(s8[4718592]{0:T(1024)(128)(4,1)} %bitcast.262), calls=%async_computation.4 | async-start | bytes 8388608
  346.7 8.5 %collective-permute-start.30 = (bf16[2,48,768]{2,1,0:T(8,128)(2,1)S(1)}, bf16[2,48,768]{2,1,0:T(8,128)(2,1)S(1)}, u32[]{:S(2)}, u32[]{:S(2)}) collective-permute-start(bf16[2,48,768]{2,1,0:T(8,128)(2,1)S(1)} %get-tuple-element.183), channel_id=1, source_target_pairs={{0,24},{4,28},{8,16},{12,20},{16,8},{20,12},{24,0},{28,4},{1,25},{... | collective-permute-start | bytes 442376 | tf_op jit(solution)/shard_map/ppermute | solution.py:359
  351.4 9.9 %collective-permute-start.18 = (bf16[2,4,48,768]{3,2,1,0:T(8,128)(2,1)S(1)}, bf16[2,4,48,768]{3,2,1,0:T(8,128)(2,1)S(1)}, u32[]{:S(2)}, u32[]{:S(2)}) collective-permute-start(bf16[2,4,48,768]{3,2,1,0:T(8,128)(2,1)S(1)} %dynamic-slice_bitcast_fusion.5), channel_id=1, source_target_pairs={{0,4},{4,0},{8,12},{12,8},{16,20},{20,16},{24,28},{28,24},{1,5},{5... | collective-permute-start | bytes 1769480 | tf_op jit(solution)/shard_map/ppermute | solution.py:359
  352.6 6.0 %collective-permute-start.29 = (bf16[2,48,768]{2,1,0:T(8,128)(2,1)S(1)}, bf16[2,48,768]{2,1,0:T(8,128)(2,1)S(1)}, u32[]{:S(2)}, u32[]{:S(2)}) collective-permute-start(bf16[2,48,768]{2,1,0:T(8,128)(2,1)S(1)} %get-tuple-element.182), channel_id=1, source_target_pairs={{0,16},{4,20},{8,24},{12,28},{16,0},{20,4},{24,8},{28,12},{1,17},{... | collective-permute-start | bytes 442376 | tf_op jit(solution)/shard_map/ppermute | solution.py:359
  355.2 5.4 %collective-permute-start.28 = (bf16[2,48,768]{2,1,0:T(8,128)(2,1)S(1)}, bf16[2,48,768]{2,1,0:T(8,128)(2,1)S(1)}, u32[]{:S(2)}, u32[]{:S(2)}) collective-permute-start(bf16[2,48,768]{2,1,0:T(8,128)(2,1)S(1)} %get-tuple-element.181), channel_id=1, source_target_pairs={{0,8},{4,12},{8,0},{12,4},{16,24},{20,28},{24,16},{28,20},{1,9},{5... | collective-permute-start | bytes 442376 | tf_op jit(solution)/shard_map/ppermute | solution.py:359
  355.3 18.8 %slice-start.1 = ((s8[4718592]{0:T(1024)(128)(4,1)}), s8[524288]{0:T(1024)(128)(4,1)S(1)}, s32[]{:S(2)}) async-start(s8[4718592]{0:T(1024)(128)(4,1)} %bitcast.262), calls=%async_computation.5 | async-start | bytes 1048576
  358.6 11.1 %collective-permute-start.16 = (bf16[4,2,48,768]{3,2,0,1:T(8,128)(2,1)S(1)}, bf16[4,2,48,768]{3,2,0,1:T(8,128)(2,1)S(1)}, u32[]{:S(2)}, u32[]{:S(2)}) collective-permute-start(bf16[4,2,48,768]{3,2,0,1:T(8,128)(2,1)S(1)} %bitcast.288), channel_id=1, source_target_pairs={{0,2},{1,3},{2,0},{3,1},{4,6},{5,7},{6,4},{7,5},{8,10},{9,11},{10,... | collective-permute-start | bytes 1769480 | tf_op jit(solution)/shard_map/ppermute | solution.py:359
  361.5 12.5 %collective-permute-start.19 = (bf16[4,48,768]{2,1,0:T(8,128)(2,1)S(1)}, bf16[4,48,768]{2,1,0:T(8,128)(2,1)S(1)}, u32[]{:S(2)}, u32[]{:S(2)}) collective-permute-start(bf16[4,48,768]{2,1,0:T(8,128)(2,1)S(1)} %slice_bitcast_fusion.8), channel_id=1, source_target_pairs={{0,2},{1,3},{2,0},{3,1},{4,6},{5,7},{6,4},{7,5},{8,10},{9,11},{10,... | collective-permute-start | bytes 884744 | tf_op jit(solution)/shard_map/ppermute | solution.py:359
  369.9 10.6 %collective-permute-start.17 = (bf16[4,48,768]{2,1,0:T(8,128)(2,1)S(1)}, bf16[4,48,768]{2,1,0:T(8,128)(2,1)S(1)}, u32[]{:S(2)}, u32[]{:S(2)}) collective-permute-start(bf16[4,48,768]{2,1,0:T(8,128)(2,1)S(1)} %dynamic-slice_bitcast_fusion.7), channel_id=1, source_target_pairs={{0,4},{4,0},{8,12},{12,8},{16,20},{20,16},{24,28},{28,24},{1,5},{5... | collective-permute-start | bytes 884744 | tf_op jit(solution)/shard_map/ppermute | solution.py:359
  378.4 19.8 %collective-permute-start.40 = (bf16[4,2,96,768]{3,2,1,0:T(8,128)(2,1)S(1)}, bf16[4,2,96,768]{3,2,1,0:T(8,128)(2,1)S(1)}, u32[]{:S(2)}, u32[]{:S(2)}) collective-permute-start(bf16[4,2,96,768]{3,2,1,0:T(8,128)(2,1)S(1)} %bitcast.280), channel_id=1, source_target_pairs={{0,2},{1,3},{2,0},{3,1},{4,6},{5,7},{6,4},{7,5},{8,10},{9,11},{10,... | collective-permute-start | bytes 3538952 | tf_op jit(solution)/shard_map/ppermute | solution.py:359
  380.6 7.1 %collective-permute-start.22 = (bf16[2,48,768]{2,1,0:T(8,128)(2,1)S(1)}, bf16[2,48,768]{2,1,0:T(8,128)(2,1)S(1)}, u32[]{:S(2)}, u32[]{:S(2)}) collective-permute-start(bf16[2,48,768]{2,1,0:T(8,128)(2,1)S(1)} %get-tuple-element.180), channel_id=1, source_target_pairs={{0,24},{4,28},{8,16},{12,20},{16,8},{20,12},{24,0},{28,4},{1,25},{... | collective-permute-start | bytes 442376 | tf_op jit(solution)/shard_map/ppermute | solution.py:359
  383.5 7.3 %collective-permute-start.21 = (bf16[2,48,768]{2,1,0:T(8,128)(2,1)S(1)}, bf16[2,48,768]{2,1,0:T(8,128)(2,1)S(1)}, u32[]{:S(2)}, u32[]{:S(2)}) collective-permute-start(bf16[2,48,768]{2,1,0:T(8,128)(2,1)S(1)} %get-tuple-element.179), channel_id=1, source_target_pairs={{0,16},{4,20},{8,24},{12,28},{16,0},{20,4},{24,8},{28,12},{1,17},{... | collective-permute-start | bytes 442376 | tf_op jit(solution)/shard_map/ppermute | solution.py:359
  383.5 7.3 %collective-permute-start.20 = (bf16[2,48,768]{2,1,0:T(8,128)(2,1)S(1)}, bf16[2,48,768]{2,1,0:T(8,128)(2,1)S(1)}, u32[]{:S(2)}, u32[]{:S(2)}) collective-permute-start(bf16[2,48,768]{2,1,0:T(8,128)(2,1)S(1)} %get-tuple-element.178), channel_id=1, source_target_pairs={{0,8},{4,12},{8,0},{12,4},{16,24},{20,28},{24,16},{28,20},{1,9},{5... | collective-permute-start | bytes 442376 | tf_op jit(solution)/shard_map/ppermute | solution.py:359
  390.8 11.0 %slice-start.2 = ((s8[4718592]{0:T(1024)(128)(4,1)}), s8[4194304]{0:T(1024)(128)(4,1)S(1)}, s32[]{:S(2)}) async-start(s8[4718592]{0:T(1024)(128)(4,1)} %bitcast.264), calls=%async_computation.6 | async-start | bytes 8388608
  390.9 10.9 %slice-start.3 = ((s8[4718592]{0:T(1024)(128)(4,1)}), s8[524288]{0:T(1024)(128)(4,1)S(1)}, s32[]{:S(2)}) async-start(s8[4718592]{0:T(1024)(128)(4,1)} %bitcast.264), calls=%async_computation.7 | async-start | bytes 1048576
  391.2 28.9 %collective-permute-start.42 = (bf16[2,4,96,768]{3,2,1,0:T(8,128)(2,1)S(1)}, bf16[2,4,96,768]{3,2,1,0:T(8,128)(2,1)S(1)}, u32[]{:S(2)}, u32[]{:S(2)}) collective-permute-start(bf16[2,4,96,768]{3,2,1,0:T(8,128)(2,1)S(1)} %dynamic-slice_bitcast_fusion), channel_id=1, source_target_pairs={{0,4},{4,0},{8,12},{12,8},{16,20},{20,16},{24,28},{28,24},{1,5},{5... | collective-permute-start | bytes 3538952 | tf_op jit(solution)/shard_map/ppermute | solution.py:359
  398.6 34.3 %collective-permute-start.41 = (bf16[4,96,768]{2,1,0:T(8,128)(2,1)S(1)}, bf16[4,96,768]{2,1,0:T(8,128)(2,1)}, u32[]{:S(2)}, u32[]{:S(2)}) collective-permute-start(bf16[4,96,768]{2,1,0:T(8,128)(2,1)S(1)} %dynamic-slice_bitcast_fusion.2), channel_id=1, source_target_pairs={{0,4},{4,0},{8,12},{12,8},{16,20},{20,16},{24,28},{28,24},{1,5},{5... | collective-permute-start | bytes 1769480 | tf_op jit(solution)/shard_map/ppermute | solution.py:359
  406.1 34.7 %collective-permute-start.32 = (bf16[4,2,96,768]{3,2,1,0:T(8,128)(2,1)S(1)}, bf16[4,2,96,768]{3,2,1,0:T(8,128)(2,1)S(1)}, u32[]{:S(2)}, u32[]{:S(2)}) collective-permute-start(bf16[4,2,96,768]{3,2,1,0:T(8,128)(2,1)S(1)} %bitcast.281), channel_id=1, source_target_pairs={{0,2},{1,3},{2,0},{3,1},{4,6},{5,7},{6,4},{7,5},{8,10},{9,11},{10,... | collective-permute-start | bytes 3538952 | tf_op jit(solution)/shard_map/ppermute | solution.py:359
  420.5 15.6 %collective-permute-start.43 = (bf16[4,96,768]{2,1,0:T(8,128)(2,1)S(1)}, bf16[4,96,768]{2,1,0:T(8,128)(2,1)S(1)}, u32[]{:S(2)}, u32[]{:S(2)}) collective-permute-start(bf16[4,96,768]{2,1,0:T(8,128)(2,1)S(1)} %slice_bitcast_fusion), channel_id=1, source_target_pairs={{0,2},{1,3},{2,0},{3,1},{4,6},{5,7},{6,4},{7,5},{8,10},{9,11},{10,... | collective-permute-start | bytes 1769480 | tf_op jit(solution)/shard_map/ppermute | solution.py:359
  421.6 31.1 %collective-permute-start.34 = (bf16[2,4,96,768]{3,2,1,0:T(8,128)(2,1)S(1)}, bf16[2,4,96,768]{3,2,1,0:T(8,128)(2,1)S(1)}, u32[]{:S(2)}, u32[]{:S(2)}) collective-permute-start(bf16[2,4,96,768]{3,2,1,0:T(8,128)(2,1)S(1)} %dynamic-slice_bitcast_fusion.1), channel_id=1, source_target_pairs={{0,4},{4,0},{8,12},{12,8},{16,20},{20,16},{24,28},{28,24},{1,5},{5... | collective-permute-start | bytes 3538952 | tf_op jit(solution)/shard_map/ppermute | solution.py:359
  436.3 18.7 %collective-permute-start.46 = (bf16[2,96,768]{2,1,0:T(8,128)(2,1)S(1)}, bf16[2,96,768]{2,1,0:T(8,128)(2,1)S(1)}, u32[]{:S(2)}, u32[]{:S(2)}) collective-permute-start(bf16[2,96,768]{2,1,0:T(8,128)(2,1)S(1)} %get-tuple-element.173), channel_id=1, source_target_pairs={{0,24},{4,28},{8,16},{12,20},{16,8},{20,12},{24,0},{28,4},{1,25},{... | collective-permute-start | bytes 884744 | tf_op jit(solution)/shard_map/ppermute | solution.py:359
  439.9 24.6 %collective-permute-start.45 = (bf16[2,96,768]{2,1,0:T(8,128)(2,1)S(1)}, bf16[2,96,768]{2,1,0:T(8,128)(2,1)S(1)}, u32[]{:S(2)}, u32[]{:S(2)}) collective-permute-start(bf16[2,96,768]{2,1,0:T(8,128)(2,1)S(1)} %get-tuple-element.172), channel_id=1, source_target_pairs={{0,16},{4,20},{8,24},{12,28},{16,0},{20,4},{24,8},{28,12},{1,17},{... | collective-permute-start | bytes 884744 | tf_op jit(solution)/shard_map/ppermute | solution.py:359
  439.9 24.6 %collective-permute-start.44 = (bf16[2,96,768]{2,1,0:T(8,128)(2,1)S(1)}, bf16[2,96,768]{2,1,0:T(8,128)(2,1)S(1)}, u32[]{:S(2)}, u32[]{:S(2)}) collective-permute-start(bf16[2,96,768]{2,1,0:T(8,128)(2,1)S(1)} %get-tuple-element.171), channel_id=1, source_target_pairs={{0,8},{4,12},{8,0},{12,4},{16,24},{20,28},{24,16},{28,20},{1,9},{5... | collective-permute-start | bytes 884744 | tf_op jit(solution)/shard_map/ppermute | solution.py:359
  441.1 23.6 %collective-permute-start.33 = (bf16[4,96,768]{2,1,0:T(8,128)(2,1)S(1)}, bf16[4,96,768]{2,1,0:T(8,128)(2,1)S(1)}, u32[]{:S(2)}, u32[]{:S(2)}) collective-permute-start(bf16[4,96,768]{2,1,0:T(8,128)(2,1)S(1)} %dynamic-slice_bitcast_fusion.3), channel_id=1, source_target_pairs={{0,4},{4,0},{8,12},{12,8},{16,20},{20,16},{24,28},{28,24},{1,5},{5... | collective-permute-start | bytes 1769480 | tf_op jit(solution)/shard_map/ppermute | solution.py:359
  453.2 11.7 %collective-permute-start.35 = (bf16[4,96,768]{2,1,0:T(8,128)(2,1)S(1)}, bf16[4,96,768]{2,1,0:T(8,128)(2,1)S(1)}, u32[]{:S(2)}, u32[]{:S(2)}) collective-permute-start(bf16[4,96,768]{2,1,0:T(8,128)(2,1)S(1)} %slice_bitcast_fusion.2), channel_id=1, source_target_pairs={{0,2},{1,3},{2,0},{3,1},{4,6},{5,7},{6,4},{7,5},{8,10},{9,11},{10,... | collective-permute-start | bytes 1769480 | tf_op jit(solution)/shard_map/ppermute | solution.py:359
  465.1 8.8 %collective-permute-start.38 = (bf16[2,96,768]{2,1,0:T(8,128)(2,1)S(1)}, bf16[2,96,768]{2,1,0:T(8,128)(2,1)S(1)}, u32[]{:S(2)}, u32[]{:S(2)}) collective-permute-start(bf16[2,96,768]{2,1,0:T(8,128)(2,1)S(1)} %get-tuple-element.170), channel_id=1, source_target_pairs={{0,24},{4,28},{8,16},{12,20},{16,8},{20,12},{24,0},{28,4},{1,25},{... | collective-permute-start | bytes 884744 | tf_op jit(solution)/shard_map/ppermute | solution.py:359
  465.6 15.8 %collective-permute-start.37 = (bf16[2,96,768]{2,1,0:T(8,128)(2,1)S(1)}, bf16[2,96,768]{2,1,0:T(8,128)(2,1)S(1)}, u32[]{:S(2)}, u32[]{:S(2)}) collective-permute-start(bf16[2,96,768]{2,1,0:T(8,128)(2,1)S(1)} %get-tuple-element.169), channel_id=1, source_target_pairs={{0,16},{4,20},{8,24},{12,28},{16,0},{20,4},{24,8},{28,12},{1,17},{... | collective-permute-start | bytes 884744 | tf_op jit(solution)/shard_map/ppermute | solution.py:359
  466.1 15.3 %collective-permute-start.36 = (bf16[2,96,768]{2,1,0:T(8,128)(2,1)S(1)}, bf16[2,96,768]{2,1,0:T(8,128)(2,1)S(1)}, u32[]{:S(2)}, u32[]{:S(2)}) collective-permute-start(bf16[2,96,768]{2,1,0:T(8,128)(2,1)S(1)} %get-tuple-element.168), channel_id=1, source_target_pairs={{0,8},{4,12},{8,0},{12,4},{16,24},{20,28},{24,16},{28,20},{1,9},{5... | collective-permute-start | bytes 884744 | tf_op jit(solution)/shard_map/ppermute | solution.py:359
  (18 other events, 67.5 us)
